TPU v7x, 32 devices: a whole 2x2x4 slice. The times are simulated.
32 devices in a mesh: dp: 2 (over x), tp: 4 (over z), pp: 4 (over y, core).
Axes of the slice: x: 2, y: 2, z: 4, core: 2. Of those that a mesh axis runs over, the one named last changes fastest.
Arguments:
- tok_ids: int32 [8, 1, 512], P(('dp', 'pp')), parts along dimension 0
- hid_in: bfloat16 [8, 1, 512, 128], P(('dp', 'pp')), parts along dimension 0
- cot_in: bfloat16 [8, 1, 512, 128], P(('dp', 'pp')), parts along dimension 0
- ln_gamma: float32 [8, 128], P(('dp', 'pp')), parts along dimension 0
- ln_beta: float32 [8, 128], P(('dp', 'pp')), parts along dimension 0
- emb_table: bfloat16 [8, 50304, 128], P(('dp', 'pp'), 'tp'), parts along dimension 0
- w_in: bfloat16 [8, 128, 512], P(('dp', 'pp'), None, 'tp'), parts along dimension 0
- b_in: float32 [8, 512], P(('dp', 'pp'), 'tp'), parts along dimension 0
- w_out: bfloat16 [8, 512, 128], P(('dp', 'pp'), 'tp'), parts along dimension 0
Outputs:
- output 1: float32 [8, 50304, 128], P(('dp', 'pp'), 'tp'), parts along dimension 0
- output 2: float32 [8], P(('dp', 'pp')), parts along dimension 0
- output 3: float32 [8, 128], P(('dp', 'pp')), parts along dimension 0
- output 4: float32 [8, 128], P(('dp', 'pp')), parts along dimension 0
- output 5: float32 [8, 128, 512], P(('dp', 'pp'), None, 'tp'), parts along dimension 0
- output 6: float32 [8, 512], P(('dp', 'pp'), 'tp'), parts along dimension 0
- output 7: float32 [8, 512, 128], P(('dp', 'pp'), 'tp'), parts along dimension 0
There are 2 independent parts. A program takes and returns all parts, laid end to end along the dimension named above; each array names one.
All inputs are finite; a program needn't handle non-finite values.
Results may differ from a plain program's by a relative error of at most 0.00333534.
Values sent between devices are 32-bit elements.
A program may use at most 1 GiB of HBM per device.

v0:
```python
import jax
import jax.numpy as jnp
from jax import lax
from jax.sharding import PartitionSpec as P

LN_EPS = 1e-5
CONTRACT_LAST = (((1,), (1,)), ((), ()))
CONTRACT_FIRST = (((0,), (0,)), ((), ()))


def ln_forward(rows_f):
    centre = rows_f - jnp.mean(rows_f, axis=-1, keepdims=True)
    inv_std = lax.rsqrt(jnp.mean(centre * centre, axis=-1, keepdims=True) + LN_EPS)
    return centre * inv_std, inv_std


def ln_input_grad(x_hat, inv_std, ln_gain, d_out):
    value_a6 = d_out * ln_gain
    return inv_std * (value_a6 - jnp.mean(value_a6, axis=-1, keepdims=True) - x_hat * jnp.mean(value_a6 * x_hat, axis=-1, keepdims=True))


def gelu_tanh(values):
    return jax.nn.gelu(values, approximate=True)


def solution(mesh):
    stages = mesh.shape['pp']
    lead_axes = ('dp', 'pp')
    end_pairs = [(0, stages - 1), (stages - 1, 0)]

    def body(tok_ids, hid_in, cot_in, ln_gamma, ln_beta, emb_table, w_in, b_in, w_out):
        stage_idx = lax.axis_index('pp')
        tp_rank = lax.axis_index('tp')
        stage_kind = jnp.where(stage_idx == 0, 0, jnp.where(stage_idx == stages - 1, 2, 1))
        model_dim = hid_in.shape[-1]
        ids_flat = tok_ids.reshape(-1)
        tokens = ids_flat.shape[0]
        hid_rows = hid_in.reshape(tokens, model_dim)
        cot_rows = cot_in.reshape(tokens, model_dim)
        ln_gain = ln_gamma[0]
        ln_shift = ln_beta[0]
        vocab_tab = emb_table[0]
        w_first = w_in[0]
        bias_first = b_in[0]
        w_second = w_out[0]
        vocab_local = vocab_tab.shape[0]
        ff_local = w_first.shape[1]
        local_ids = ids_flat - tp_rank * vocab_local
        in_shard = (local_ids >= 0) & (local_ids < vocab_local)
        zero_rows = jnp.zeros((tokens, model_dim), jnp.float32)
        unit_col = jnp.ones((tokens, 1), jnp.float32)
        zero_norm = jnp.zeros((tokens, model_dim), jnp.bfloat16)
        zero_probs = jnp.zeros((tokens, vocab_local), jnp.float32)
        zero_stats = jnp.zeros((tokens, 3), jnp.float32)
        zero_w1 = jnp.zeros((model_dim, ff_local), jnp.float32)
        zero_b1 = jnp.zeros((ff_local,), jnp.float32)
        zero_w2 = jnp.zeros((ff_local, model_dim), jnp.float32)
        zero_vec = jnp.zeros((model_dim,), jnp.float32)
        zero_tab = jnp.zeros((vocab_local, model_dim), jnp.float32)
        zero_loss = jnp.zeros((), jnp.float32)

        def first_lookup():
            picked = vocab_tab[jnp.where(in_shard, local_ids, 0)]
            looked = jnp.where(in_shard[:, None], picked, 0).astype(jnp.float32)
            return (looked, zero_rows, unit_col, zero_norm, zero_probs, zero_stats, zero_w1, zero_b1, zero_w2)

        def middle_mlp():
            x_mid, inv_mid = ln_forward(hid_rows.astype(jnp.float32))
            norm_mid = (x_mid * ln_gain + ln_shift).astype(jnp.bfloat16)
            pre_act = jnp.dot(norm_mid, w_first, preferred_element_type=jnp.float32) + bias_first
            act_val, gelu_back = jax.vjp(gelu_tanh, pre_act)
            w2_part = lax.dot_general(act_val.astype(jnp.bfloat16), cot_rows, CONTRACT_FIRST, preferred_element_type=jnp.float32)
            d_act = lax.dot_general(cot_rows, w_second, CONTRACT_LAST, preferred_element_type=jnp.float32)
            d_pre = gelu_back(d_act)[0]
            d_pre_b = d_pre.astype(jnp.bfloat16)
            w1_part = lax.dot_general(norm_mid, d_pre_b, CONTRACT_FIRST, preferred_element_type=jnp.float32)
            dh_part = lax.dot_general(d_pre_b, w_first, CONTRACT_LAST, preferred_element_type=jnp.float32)
            return (dh_part, x_mid, inv_mid, zero_norm, zero_probs, zero_stats, w1_part, jnp.sum(d_pre, axis=0), w2_part)

        def last_head():
            x_last, inv_last = ln_forward(hid_rows.astype(jnp.float32))
            norm_last = (x_last * ln_gain + ln_shift).astype(jnp.bfloat16)
            logits = lax.dot_general(norm_last, vocab_tab, CONTRACT_LAST, preferred_element_type=jnp.float32)
            local_top = jnp.max(logits, axis=-1, keepdims=True)
            exp_vals = jnp.exp(logits - local_top)
            label_hit = jnp.arange(vocab_local)[None, :] == local_ids[:, None]
            local_target = jnp.sum(jnp.where(label_hit, logits, 0.0), axis=-1, keepdims=True)
            row_stats = jnp.concatenate([local_top, jnp.sum(exp_vals, axis=-1, keepdims=True), local_target], axis=-1)
            return (zero_rows, x_last, inv_last, norm_last, exp_vals, row_stats, zero_w1, zero_b1, zero_w2)

        phase_one = lax.switch(stage_kind, [first_lookup, middle_mlp, last_head])
        rows_part, x_hat, inv_std, normed_b, exp_local, row_stats, w1_grad, b1_grad, w2_grad = phase_one
        rows_sum = lax.psum(rows_part, 'tp')
        stats_all = lax.all_gather(row_stats, 'tp')

        def first_backward():
            x_first, inv_first = ln_forward(rows_sum)
            d_out = cot_rows.astype(jnp.float32)
            d_rows = ln_input_grad(x_first, inv_first, ln_gain, d_out).astype(jnp.bfloat16).astype(jnp.float32)
            seg_ids = jnp.where(in_shard, local_ids, vocab_local)
            tab_part = jax.ops.segment_sum(d_rows, seg_ids, num_segments=vocab_local)
            return (tab_part, zero_rows, jnp.sum(d_out * x_first, axis=0), jnp.sum(d_out, axis=0), zero_loss)

        def middle_none():
            return (zero_tab, zero_rows, zero_vec, zero_vec, zero_loss)

        def last_backward():
            glob_top = jnp.max(stats_all[:, :, 0], axis=0)
            glob_sum = jnp.sum(stats_all[:, :, 1] * jnp.exp(stats_all[:, :, 0] - glob_top), axis=0)
            glob_target = jnp.sum(stats_all[:, :, 2], axis=0)
            loss_mean = jnp.mean(jnp.log(glob_sum) + glob_top - glob_target)
            prob_scale = (jnp.exp(row_stats[:, 0] - glob_top) / glob_sum)[:, None]
            label_hit = jnp.arange(vocab_local)[None, :] == local_ids[:, None]
            grad_logits = (exp_local * prob_scale - label_hit.astype(jnp.float32)).astype(jnp.bfloat16)
            tab_part = lax.dot_general(grad_logits, normed_b, CONTRACT_FIRST, preferred_element_type=jnp.float32)
            d_local = jnp.dot(grad_logits, vocab_tab, preferred_element_type=jnp.float32)
            return (tab_part, d_local, zero_vec, zero_vec, loss_mean)

        tab_grad, d_part, first_gain, first_shift, loss_val = lax.switch(stage_kind, [first_backward, middle_none, last_backward])
        d_sum = lax.psum(d_part, 'tp')
        recv_grad = lax.ppermute(tab_grad, 'pp', end_pairs)
        tied_grad = tab_grad + recv_grad
        d_normed = jnp.where(stage_kind == 1, rows_sum, d_sum)
        gamma_grad = jnp.where(stage_kind == 0, first_gain, jnp.sum(d_normed * x_hat, axis=0))
        beta_grad = jnp.where(stage_kind == 0, first_shift, jnp.sum(d_normed, axis=0))
        return (tied_grad[None], loss_val[None], gamma_grad[None], beta_grad[None], w1_grad[None], b1_grad[None], w2_grad[None])

    specs_in = (P(lead_axes, None, None), P(lead_axes, None, None, None), P(lead_axes, None, None, None), P(lead_axes, None), P(lead_axes, None), P(lead_axes, 'tp', None), P(lead_axes, None, 'tp'), P(lead_axes, 'tp'), P(lead_axes, 'tp', None))
    specs_out = (P(lead_axes, 'tp', None), P(lead_axes), P(lead_axes, None), P(lead_axes, None), P(lead_axes, None, 'tp'), P(lead_axes, 'tp'), P(lead_axes, 'tp', None))
    return jax.shard_map(body, mesh=mesh, in_specs=specs_in, out_specs=specs_out, check_vma=False)
```

profile of v0, /device:TPU:7, one launch (start us, length us, event | category | flops | bytes accessed | tf_op | source)
XLA Modules:
  0.0 202.6 jit_solution(10533939178033258799)
XLA Ops:
  7.2 0.0 all-reduce.3.cloned.1.call-start
  7.2 0.7 broadcast_subtract_fusion
  7.9 45.5 %conditional.2 = (f32[512,128]{1,0:T(8,128)S(1)}, f32[512,128]{1,0:T(8,128)}, bf16[512,128]{1,0:T(8,128)(2,1)S(1)}, f32[512,12576]{1,0:T(8,128)}, f32[512,3]{1,0...) conditional(s32[]{:T(128)} %clamp.4, ...), branch_computations={%region_0.1_spmd, %region_1.5_spmd, %region_5.11_spmd} | conditional | flops 1687783424 | bytes 134411904 | solution.py:91
  7.9 1.0 convert_reduce_fusion.1
  8.9 1.1 fusion.28
  10.1 1.8 add_convert_fusion.3
  11.9 5.7 %select_reduce_fusion = (f32[512]{0:T(512)S(1)}, f32[512]{0:T(512)S(1)}, f32[512,12576]{0,1:T(8,128)S(1)}) fusion(s32[512]{0:T(512)S(1)} %get-tuple-element.71, bf16[512,128]{1,0:T(8,128)(2,1)S(1)} %get-tuple-element.192, bf16[12576,128]{1,0:T(8,128)(2,1)} %get-tuple-element.70), kind=kOutput, calls=%fused_computation.37 | convolution fusion | flops 1674116096 | bytes 29112320 | tf_op jit(solution)/shard_map/cond/branch_2_fun/dot_general | solution.py:83
  17.6 9.5 %fusion.54 = (f32[512]{0:T(512)S(1)}, f32[512,12576]{0,1:T(8,128)}) fusion(f32[512,12576]{0,1:T(8,128)S(1)} %get-tuple-element.169, f32[512]{0:T(512)S(1)} %get-tuple-element.152), kind=kLoop, calls=%fused_computation.101 | loop fusion | flops 12877312 | bytes 51515392 | tf_op jit(solution)/shard_map/cond/branch_2_fun/reduce_sum | solution.py:88
  27.1 0.1 copy.23
  27.3 26.0 %copy.22 = f32[512,12576]{1,0:T(8,128)} copy(f32[512,12576]{0,1:T(8,128)} %get-tuple-element.162) | data formatting | bytes 51511296 | tf_op jit(solution)/shard_map
  53.4 0.0 copy-start.5
  53.4 0.0 copy-start.6
  53.4 0.0 copy-start.7
  53.4 0.7 copy-done
  54.1 0.0 all-reduce.3.cloned.1.call-update
  54.1 0.0 all-reduce.5.cloned.1.call-start
  54.2 19.0 %all-gather = f32[2048,3]{1,0:T(8,128)S(1)} all-gather(f32[512,3]{1,0:T(8,128)S(1)} %get-tuple-element.104), channel_id=2, replica_groups=mesh['dp'=2,'tp'=4,'pp'=4] {'tp'}, dimensions={0}, use_global_device_ids=true | all-gather | bytes 30720 | tf_op jit(solution)/shard_map/all_gather | solution.py:94
  73.2 16.6 %all-reduce.3.cloned.1.call-done = f32[512,128]{1,0:T(8,128)} async-done(((f32[512,128]{1,0:T(8,128)}), f32[512,128]{1,0:T(8,128)}) %all-reduce.3.cloned.1.call-update) | async-done | bytes 262160 | tf_op jit(solution)/shard_map/psum | solution.py:93
  89.7 23.1 %conditional.3 = (f32[12576,128]{1,0:T(8,128)}, f32[512,128]{1,0:T(8,128)S(1)}, f32[128]{0:T(128)S(1)}, f32[128]{0:T(128)S(1)}, f32[]{:T(128)}) conditional(s32[]{:T(128)} %clamp.4, (pred[512]{0:T(512)(128)(4,1)S(1)}, s32[512]{0:T(512)S(1)}, f32[512,128]{1,0:T(8,128)}, bf16[512,128]{1,0:T(8,128)(2,1)}, ...), branch_computations={%region_12.20_spmd, %region_20.21_spmd, %region_21.26_spmd} | conditional | flops 3328928768 | bytes 87440472 | solution.py:119
  89.8 0.3 copy.27
  90.2 0.6 subtract_reduce_fusion
  91.4 0.1 copy.25
  91.6 12.2 %subtract_convert_fusion = bf16[512,12576]{1,0:T(8,128)(2,1)S(1)} fusion(f32[512,12576]{1,0:T(8,128)} %get-tuple-element.77, s32[512]{0:T(512)S(1)} %get-tuple-element.80, f32[512]{0:T(512)S(1)} %bitcast.85), kind=kLoop, calls=%fused_computation.49 | loop fusion | flops 32194560 | bytes 38637568 | tf_op jit(solution)/shard_map/cond/branch_2_fun/convert_element_type | solution.py:114
  103.8 5.5 %fusion.57 = f32[12576,128]{1,0:T(8,128)} fusion(bf16[512,12576]{1,0:T(8,128)(2,1)S(1)} %subtract_convert_fusion, bf16[512,128]{1,0:T(8,128)(2,1)S(1)} %get-tuple-element.81), kind=kOutput, calls=%fused_computation.103 | convolution fusion | flops 1648361472 | bytes 19447808 | tf_op jit(solution)/shard_map/cond/branch_2_fun/dot_general | solution.py:115
  109.3 3.5 %fusion.58 = f32[512,128]{1,0:T(8,128)S(1)} fusion(bf16[512,12576]{1,0:T(8,128)(2,1)S(1)} %subtract_convert_fusion, bf16[12576,128]{1,0:T(8,128)(2,1)S(1)} %copy-done.4), kind=kOutput, calls=%fused_computation.104 | convolution fusion | flops 1648361472 | bytes 16359424 | tf_op jit(solution)/shard_map/cond/branch_2_fun/dot_general | solution.py:116
  112.9 1.9 collective-permute-start
  114.8 0.0 all-reduce.5.cloned.1.call-update
  114.8 33.5 %all-reduce.5.cloned.1.call-done = f32[512,128]{1,0:T(8,128)} async-done(((f32[512,128]{1,0:T(8,128)}), f32[512,128]{1,0:T(8,128)}) %all-reduce.5.cloned.1.call-update) | async-done | bytes 262160 | tf_op jit(solution)/shard_map/psum | solution.py:120
  148.3 1.1 fusion.51
  149.4 0.5 fusion.52
  149.9 36.8 %collective-permute-done = f32[12576,128]{1,0:T(8,128)} collective-permute-done((f32[12576,128]{1,0:T(8,128)}, f32[12576,128]{1,0:T(8,128)}, u32[]{:S(2)}, u32[]{:S(2)}) %collective-permute-start) | collective-permute-done | bytes 6438944 | tf_op jit(solution)/shard_map/ppermute | solution.py:121
  186.8 7.9 %add_bitcast_fusion = f32[1,12576,128]{2,1,0:T(8,128)} fusion(f32[12576,128]{1,0:T(8,128)} %get-tuple-element.107, f32[12576,128]{1,0:T(8,128)} %collective-permute-done), kind=kLoop, calls=%fused_computation.91 | loop fusion | flops 1609728 | bytes 19316736 | tf_op jit(solution)/shard_map/broadcast_in_dim | solution.py:126
  (25 shorter events, 0.2 us)
Async XLA Ops:
  7.2 82.6 %all-reduce.3.cloned.1.call-start = ((), (), s32[]{:S(2)}) async-start(), calls=%async_computation | async-start | bytes 524288 | tf_op jit(solution)/shard_map/psum | solution.py:93
  11.9 5.7 %copy-start.2 = (bf16[512,128]{1,0:T(8,128)(2,1)}, bf16[512,128]{1,0:T(8,128)(2,1)S(1)}, u32[]{:S(2)}) copy-start(bf16[512,128]{1,0:T(8,128)(2,1)S(1)} %get-tuple-element.192) | copy-start | bytes 393220 | tf_op jit(solution)/shard_map/cond
  27.3 26.1 %copy-start.3 = (bf16[512,128]{1,0:T(8,128)(2,1)S(1)}, bf16[512,128]{1,0:T(8,128)(2,1)}, u32[]{:S(2)}) copy-start(bf16[512,128]{1,0:T(8,128)(2,1)} %copy-done.2) | copy-start | bytes 393220 | tf_op jit(solution)/shard_map/cond
  53.4 0.7 copy-start
  53.4 36.4 %copy-start.5 = (f32[1,128,128]{2,1,0:T(8,128)}, f32[1,128,128]{2,1,0:T(8,128)S(1)}, u32[]{:S(2)}) copy-start(f32[1,128,128]{2,1,0:T(8,128)S(1)} %get-tuple-element.100) | copy-start | bytes 196612
  53.4 36.3 %copy-start.6 = (f32[1,128,128]{2,1,0:T(8,128)}, f32[1,128,128]{2,1,0:T(8,128)S(1)}, u32[]{:S(2)}) copy-start(f32[1,128,128]{2,1,0:T(8,128)S(1)} %get-tuple-element.102) | copy-start | bytes 196612
  53.4 36.3 %copy-start.7 = (f32[1,128]{1,0:T(1,128)}, f32[1,128]{1,0:T(1,128)S(1)}, u32[]{:S(2)}) copy-start(f32[1,128]{1,0:T(1,128)S(1)} %get-tuple-element.101) | copy-start | bytes 1540
  54.1 94.2 %all-reduce.5.cloned.1.call-start = ((), (), s32[]{:S(2)}) async-start(), calls=%async_computation.1 | async-start | bytes 524288 | tf_op jit(solution)/shard_map/psum | solution.py:120
  103.8 5.5 %copy-start.4 = (bf16[12576,128]{1,0:T(8,128)(2,1)S(1)}, bf16[12576,128]{1,0:T(8,128)(2,1)}, u32[]{:S(2)}) copy-start(bf16[12576,128]{1,0:T(8,128)(2,1)} %get-tuple-element.82) | copy-start | bytes 9658372 | tf_op jit(solution)/shard_map/cond
  112.9 1.9 copy-start.1
  112.9 73.9 %collective-permute-start = (f32[12576,128]{1,0:T(8,128)}, f32[12576,128]{1,0:T(8,128)}, u32[]{:S(2)}, u32[]{:S(2)}) collective-permute-start(f32[12576,128]{1,0:T(8,128)} %get-tuple-element.107), channel_id=1, source_target_pairs={{0,3},{3,0},{4,7},{7,4},{8,11},{11,8},{12,15},{15,12},{16,19},{19,... | collective-permute-start | bytes 19316744 | tf_op jit(solution)/shard_map/ppermute | solution.py:121
Sparse Core Ops, SparseCore 0:
  54.2 35.4 all-reduce.2
  115.0 33.2 all-reduce.4
where the time goes:
time: 204 us; the launch traced here: 203 us
  waiting for transfers between devices  86.9 us (43%)
  other arithmetic  36.6 us (18%)
  local copies, waits for them, and re-layouts  27.3 us (13%)
  blocking collectives  19 us (9%)
  between operations  15.3 us (8%)
  matrix products  14.7 us (7%)
    ppermute x1, waiting for transfers between devices, body(): recv_grad = lax.ppermute(tab_grad, 'pp', end_pairs)  36.8 us
    psum x1, waiting for transfers between devices, body(): d_sum = lax.psum(d_part, 'tp')  33.5 us
    another operation x5, local copies, waits for them, and re-layouts  26.3 us
    all_gather x1, blocking collectives, body(): stats_all = lax.all_gather(row_stats, 'tp')  19 us
    psum x1, waiting for transfers between devices, body(): rows_sum = lax.psum(rows_part, 'tp')  16.6 us
    convert_element_type x1, other arithmetic, last_backward(): (exp_local * prob_scale - label_hit.astype(jnp.float32)).astype(jnp.bfloa...  12.2 us
    reduce_sum x1, other arithmetic, last_head(): jnp.sum(exp_vals, axis=-1, keepdims=True)  9.46 us
    broadcast_in_dim x1, other arithmetic, body(): tied_grad[None]  7.91 us
  transfers between devices with their start and end apart: 3, of which 3 were waited for; matrix products, arithmetic and copies ran while one was open for 1% of the time, Pallas kernels for 0%

commit v1 on v0

v1 whole, which is shorter than its diff:
```python
import functools

import jax
import jax.numpy as jnp
from jax import lax
from jax.experimental import pallas as pl
from jax.experimental.pallas import tpu as pltpu
from jax.sharding import PartitionSpec as P

F = jnp.float32
B = jnp.bfloat16
LN_EPS = 1e-5
LOG2E = 1.4426950408889634
LANES = 128
TILE = 256
MESH = pl.DeviceIdType.MESH
NT = (((1,), (1,)), ((), ()))
TN = (((0,), (0,)), ((), ()))


def ln_hat(rows):
    centre = rows - jnp.mean(rows, axis=-1, keepdims=True)
    inv = lax.rsqrt(jnp.mean(centre * centre, axis=-1, keepdims=True) + LN_EPS)
    return centre * inv, inv


def mm(a, b):
    return jnp.dot(a, b, preferred_element_type=F)


def lanes_row(ref, first, chunks):
    return jnp.concatenate([ref[first + c:first + c + 1, :] for c in range(chunks)], axis=1)


def stats_kernel(cfg, ids_ref, hid_ref, cot_ref, gam_ref, bet_ref, emb_hbm,
                 y_out, lab_out, lse_out, dx_out, did_out, xh_out, part_out,
                 e_ref, yt_ref, buf, pack_src, pack_dst, dx_src, dx_dst, st_src, st_all, xt_ref,
                 e_sem, send_sem, pack_sem, dx_sem, st_sem):
    stages, tps, toks, dim, vocab = cfg
    chunks = toks // LANES
    rank = lax.axis_index('tp')
    stage = lax.axis_index('pp')
    last = stages - 1
    helper = stages - 2
    e_copy = pltpu.make_async_copy(emb_hbm, e_ref, e_sem)
    full, tail = vocab // TILE - 1, vocab - (vocab // TILE - 1) * TILE

    def pack_copy(to_stage, idx):
        return pltpu.make_async_remote_copy(pack_src, pack_dst, send_sem.at[idx], pack_sem, device_id={'pp': to_stage, 'tp': rank}, device_id_type=MESH)

    def dx_copy():
        return pltpu.make_async_remote_copy(dx_src, dx_dst, send_sem.at[0], dx_sem, device_id={'pp': last, 'tp': rank}, device_id_type=MESH)

    def st_copy(to_stage, off, idx):
        return pltpu.make_async_remote_copy(st_src, st_all.at[rank], send_sem.at[idx], st_sem.at[rank], device_id={'pp': to_stage, 'tp': lax.rem(rank + off, tps)}, device_id_type=MESH)

    def signal_to(to_stage, offs):
        bar = pltpu.get_barrier_semaphore()
        for off in offs:
            pl.semaphore_signal(bar, inc=1, device_id={'pp': to_stage, 'tp': lax.rem(rank + off, tps)}, device_id_type=MESH)

    def normed(rows, gam, bet):
        hat, _ = ln_hat(rows)
        return hat, (hat * gam + bet).astype(B)

    def finish_stats():
        tops = [st_all[r, 0:chunks, :] for r in range(tps)]
        sums = [st_all[r, chunks:2 * chunks, :] for r in range(tps)]
        top = functools.reduce(jnp.maximum, tops)
        tot = functools.reduce(jnp.add, [s * jnp.exp(t - top) for s, t in zip(sums, tops)])
        lse_out[0:chunks, :] = top + jnp.log(tot)

    def unpack():
        hat, norm = normed(pack_dst[0:toks, :], pack_dst[toks + chunks:toks + chunks + 1, :], pack_dst[toks + chunks + 1:toks + chunks + 2, :])
        xh_out[...] = hat
        y_out[...] = norm
        lab_out[0:chunks, :] = pack_dst[toks:toks + chunks, :].astype(jnp.int32)

    @pl.when(stage == last)
    def _():
        e_copy.start()
        signal_to(0, range(tps))
        signal_to(helper, range(tps))
        signal_to(last, range(1, tps))
        rows = hid_ref[...].astype(F)
        pack_src[0:toks, :] = rows
        pack_src[toks:toks + chunks, :] = ids_ref[...].astype(F)
        pack_src[toks + chunks:toks + chunks + 1, :] = gam_ref[...]
        pack_src[toks + chunks + 1:toks + chunks + 2, :] = bet_ref[...]
        hat, norm = normed(rows, gam_ref[...], bet_ref[...])
        xh_out[...] = hat
        y_out[...] = norm
        lab_out[0:chunks, :] = ids_ref[...]
        yt_ref[...] = norm.astype(F).T.astype(B)
        pl.semaphore_wait(pltpu.get_barrier_semaphore(), 3 * tps - 1)
        pack_copy(0, 0).start()
        pack_copy(helper, 1).start()
        e_copy.wait()

        def logits_to(row, slot, top):
            logits = mm(e_ref[pl.ds(row, TILE), :], yt_ref[...])
            buf[slot] = logits
            return jnp.maximum(top, jnp.max(logits.reshape(TILE // 8, 8, toks), axis=0))

        def add_exp(slot, top_old, top, tot):
            ex = jnp.exp(buf[slot].reshape(TILE // 8, 8, toks) - top[None])
            return tot * jnp.exp(top_old - top) + jnp.sum(ex, axis=0)

        top0 = jnp.full((8, toks), -jnp.inf, F)
        top1 = logits_to(0, 0, top0)
        top0 = top1
        tot = jnp.zeros((8, toks), F)

        def step(i, carry):
            old, top, tot = carry
            row = pl.multiple_of(i * 2 * TILE, TILE)
            mid = logits_to(row + TILE, 1, top)
            tot = add_exp(0, old, top, tot)
            new = logits_to(row + 2 * TILE, 0, mid)
            tot = add_exp(1, top, mid, tot)
            return mid, new, tot

        pairs = (full - 2) // 2
        old, top, tot = lax.fori_loop(0, pairs, step, (top0, top1, tot), unroll=4)
        mid = logits_to((2 * pairs + 1) * TILE, 1, top)
        tot = add_exp(0, old, top, tot)
        tot = add_exp(1, top, mid, tot)
        logits = mm(e_ref[full * TILE:vocab, :], yt_ref[...]).reshape(tail // 8, 8, toks)
        new = jnp.maximum(mid, jnp.max(logits, axis=0))
        tot = tot * jnp.exp(mid - new) + jnp.sum(jnp.exp(logits - new[None]), axis=0)
        top = jnp.max(new, axis=0, keepdims=True)
        tot = jnp.sum(tot * jnp.exp(new - top), axis=0, keepdims=True)
        for c in range(chunks):
            st_src[c:c + 1, :] = top[:, c * LANES:(c + 1) * LANES]
            st_src[chunks + c:chunks + c + 1, :] = tot[:, c * LANES:(c + 1) * LANES]
        st_all[rank] = st_src[...]
        copies = []
        for to_stage, offs in ((last, range(1, tps)), (0, range(tps)), (helper, range(tps))):
            for off in offs:
                copies.append(st_copy(to_stage, off, 2 + len(copies)))
        for copy in copies:
            copy.start()
        for off in range(1, tps):
            src = lax.rem(rank + off, tps)
            pltpu.make_async_remote_copy(st_src, st_all.at[src], send_sem.at[0], st_sem.at[src], device_id={'pp': last, 'tp': rank}, device_id_type=MESH).wait_recv()
        finish_stats()
        dx_copy().wait_recv()
        dx_out[...] = dx_dst[0:toks, :].astype(B)
        did_out[0:chunks, :] = dx_dst[toks:toks + chunks, :].astype(jnp.int32)
        pack_copy(0, 0).wait_send()
        pack_copy(helper, 1).wait_send()
        for copy in copies:
            copy.wait_send()

    @pl.when(stage == 0)
    def _():
        e_copy.start()
        signal_to(last, range(tps))
        e_copy.wait()
        local = lanes_row(ids_ref, 0, chunks) - rank * vocab
        xt_ref[...] = jnp.zeros((dim, toks), F)

        def pick(row, size):
            rows = lax.broadcasted_iota(jnp.int32, (size, toks), 0) + row
            hit = jnp.where(rows == local, 1.0, 0.0).astype(B)
            xt_ref[...] += lax.dot_general(e_ref[pl.ds(row, size), :], hit, TN, preferred_element_type=F)

        def step(i, carry):
            pick(pl.multiple_of(i * TILE, TILE), TILE)
            return carry

        lax.fori_loop(0, full, step, 0, unroll=4)
        pick(full * TILE, tail)
        inside = jnp.where((local >= 0) & (local < vocab), 1.0, 0.0)
        mask = jnp.broadcast_to(inside, (LANES, toks)).T
        hat, inv = ln_hat(xt_ref[...].T)
        cot = cot_ref[...].astype(F)
        scaled = cot * gam_ref[...]
        grad = inv * (scaled - jnp.mean(scaled, axis=-1, keepdims=True) - hat * jnp.mean(scaled * hat, axis=-1, keepdims=True))
        grad = jnp.where(mask > 0.5, grad, 0.0).astype(B)
        dx_out[...] = grad
        did_out[0:chunks, :] = ids_ref[...]
        dx_src[0:toks, :] = grad.astype(F)
        dx_src[toks:toks + chunks, :] = ids_ref[...].astype(F)
        part_out[0:1, :] = jnp.sum(jnp.where(mask > 0.5, cot * hat, 0.0), axis=0, keepdims=True)
        part_out[1:2, :] = jnp.sum(jnp.where(mask > 0.5, cot, 0.0), axis=0, keepdims=True)
        pl.semaphore_wait(pltpu.get_barrier_semaphore(), tps)
        dx_copy().start()
        pack_copy(0, 0).wait_recv()
        unpack()
        for r in range(tps):
            pltpu.make_async_remote_copy(st_src, st_all.at[r], send_sem.at[0], st_sem.at[r], device_id={'pp': last, 'tp': rank}, device_id_type=MESH).wait_recv()
        finish_stats()
        dx_copy().wait_send()

    @pl.when(stage == helper)
    def _():
        signal_to(last, range(tps))
        pl.semaphore_wait(pltpu.get_barrier_semaphore(), tps)
        pack_copy(0, 0).wait_recv()
        unpack()
        for r in range(tps):
            pltpu.make_async_remote_copy(st_src, st_all.at[r], send_sem.at[0], st_sem.at[r], device_id={'pp': last, 'tp': rank}, device_id_type=MESH).wait_recv()
        finish_stats()


def grad_kernel(cfg, emb_hbm, y_ref, lab_ref, lse_ref, dx_ref, did_ref, xh_ref, pin_ref,
                hid_ref, cot_ref, gam_ref, bet_ref, w1_ref, b1_ref, w2_ref,
                emb_out, w1_out, b1_out, w2_out, part_out,
                e_ref, ya_ref, out_ref, dyt_ref, e_sem, o_sem):
    stages, tps, toks, dim, vocab = cfg
    chunks = toks // LANES
    rank = lax.axis_index('tp')
    stage = lax.axis_index('pp')
    last = stages - 1
    helper = stages - 2
    base = rank * vocab
    full, tail = vocab // TILE - 1, vocab - (vocab // TILE - 1) * TILE
    group = 8
    groups = full // group
    e_copy = pltpu.make_async_copy(emb_hbm, e_ref, e_sem)

    def out_copy(c):
        size = tail if c == groups else group * TILE
        return pltpu.make_async_copy(out_ref.at[pl.ds(c * group * TILE, size)], emb_out.at[pl.ds(c * group * TILE, size)], o_sem.at[c])

    def prepare():
        ya_ref[0:dim, :] = y_ref[...].astype(F).T.astype(B)
        lse = lanes_row(lse_ref, 0, chunks)
        hi = (lse * 0.99609375).astype(B)
        rest = lse - hi.astype(F)
        mid = rest.astype(B)
        low = (rest - mid.astype(F)).astype(B)
        pick = lax.broadcasted_iota(jnp.int32, (dim, toks), 0)
        zero = jnp.zeros((dim, toks), F)
        add = jnp.where(pick == 0, -hi.astype(F), jnp.where(pick == 1, -mid.astype(F), jnp.where(pick == 2, -low.astype(F), zero)))
        ya_ref[dim:2 * dim, :] = add.astype(B)

    def shifted(row, size):
        rows = jnp.concatenate([e_ref[pl.ds(row, size), :], jnp.ones((size, dim), B)], axis=1)
        return mm(rows, ya_ref[...])

    def zero_parts():
        w1_out[...] = jnp.zeros(w1_out.shape, F)
        b1_out[...] = jnp.zeros(b1_out.shape, F)
        w2_out[...] = jnp.zeros(w2_out.shape, F)

    @pl.when((stage == 0) | (stage == last))
    def _():
        e_copy.start()
        zero_parts()
        part_out[...] = pin_ref[...]
        prepare()
        lab = lanes_row(lab_ref, 0, chunks) - base
        did = lanes_row(did_ref, 0, chunks) - base
        e_copy.wait()

        def work(row, size):
            p = jnp.exp2(shifted(row, size) * LOG2E)
            rows = lax.broadcasted_iota(jnp.int32, (size, LANES), 0) + row
            g, h = [], []
            for c in range(chunks):
                cols = slice(c * LANES, (c + 1) * LANES)
                pc = p[:, cols]
                g.append(jnp.where(rows == lab[:, cols], pc - 1.0, pc).astype(B))
                h.append(jnp.where(rows == did[:, cols], 1.0, 0.0).astype(B))
            out_ref[pl.ds(row, size), :] = mm(jnp.concatenate(g, axis=1), y_ref[...]) + mm(jnp.concatenate(h, axis=1), dx_ref[...])

        for c in range(groups):
            def step(i, carry):
                work(pl.multiple_of(c * group * TILE + i * TILE, TILE), TILE)
                return carry
            lax.fori_loop(0, group, step, 0, unroll=4)
            out_copy(c).start()
        work(full * TILE, tail)
        out_copy(groups).start()
        for c in range(groups + 1):
            out_copy(c).wait()

    @pl.when((stage != 0) & (stage != last))
    def _():
        @pl.when(stage == helper)
        def _():
            e_copy.start()
        size = group * TILE
        out_ref[0:size, :] = jnp.zeros((size, dim), F)

        def zero_copy(c):
            n = tail if c == groups else size
            return pltpu.make_async_copy(out_ref.at[pl.ds(0, n)], emb_out.at[pl.ds(c * size, n)], o_sem.at[c])

        for c in range(groups + 1):
            zero_copy(c).start()
        hat, _ = ln_hat(hid_ref[...].astype(F))
        norm = (hat * gam_ref[...] + bet_ref[...]).astype(B)
        pre = mm(norm, w1_ref[...]) + b1_ref[...]
        cube = 0.7978845608028654 * (pre + 0.044715 * (pre * pre * pre))
        th = jnp.tanh(cube)
        act = pre * (0.5 * (1.0 + th))
        slope = 0.5 * (1.0 + th) + pre * (0.5 * (1.0 - th * th)) * (0.7978845608028654 * (1.0 + 3 * 0.044715 * pre * pre))
        w2_out[...] = lax.dot_general(act.astype(B), cot_ref[...], TN, preferred_element_type=F)
        d_act = lax.dot_general(cot_ref[...], w2_ref[...], NT, preferred_element_type=F)
        d_pre = d_act * slope
        d_b = d_pre.astype(B)
        w1_out[...] = lax.dot_general(norm, d_b, TN, preferred_element_type=F)
        b1_out[...] = jnp.sum(d_pre, axis=0, keepdims=True)
        d_h = lax.dot_general(d_b, w1_ref[...], NT, preferred_element_type=F)
        part_out[0:1, :] = jnp.sum(d_h * hat, axis=0, keepdims=True)
        part_out[1:2, :] = jnp.sum(d_h, axis=0, keepdims=True)

        @pl.when(stage == helper)
        def _():
            prepare()
            lab = lanes_row(lab_ref, 0, chunks) - base
            dyt_ref[...] = jnp.zeros((dim, toks), F)
            e_copy.wait()

            def work(row, size, loss):
                x = shifted(row, size)
                p = jnp.exp2(x * LOG2E)
                rows = lax.broadcasted_iota(jnp.int32, (size, LANES), 0) + row
                g, picked = [], []
                for c in range(chunks):
                    cols = slice(c * LANES, (c + 1) * LANES)
                    hit = rows == lab[:, cols]
                    pc = p[:, cols]
                    g.append(jnp.where(hit, pc - 1.0, pc).astype(B))
                    picked.append(jnp.sum(jnp.where(hit, x[:, cols], 0.0).reshape(size // 8, 8, LANES), axis=0))
                dyt_ref[...] += lax.dot_general(e_ref[pl.ds(row, size), :], jnp.concatenate(g, axis=1), TN, preferred_element_type=F)
                return loss + functools.reduce(jnp.add, picked)

            def step(i, loss):
                return work(pl.multiple_of(i * TILE, TILE), TILE, loss)

            loss = lax.fori_loop(0, full, step, jnp.zeros((8, LANES), F), unroll=4)
            loss = work(full * TILE, tail, loss)
            dy = dyt_ref[...].T
            part_out[2:3, :] = jnp.sum(dy * xh_ref[...], axis=0, keepdims=True)
            part_out[3:4, :] = jnp.sum(dy, axis=0, keepdims=True)
            part_out[4:5, :] = jnp.sum(loss, axis=0, keepdims=True)

        for c in range(groups + 1):
            zero_copy(c).wait()


def sum_kernel(cfg, part_ref, out_ref, got, send_sem, recv_sem):
    stages, tps, toks, dim, vocab = cfg
    rank = lax.axis_index('tp')
    stage = lax.axis_index('pp')
    last = stages - 1
    helper = stages - 2
    bar = pltpu.get_barrier_semaphore()

    def copy_to(to_stage, off, idx):
        return pltpu.make_async_remote_copy(part_ref, got.at[rank], send_sem.at[idx], recv_sem.at[rank], device_id={'pp': to_stage, 'tp': lax.rem(rank + off, tps)}, device_id_type=MESH)

    def arrived(src):
        return pltpu.make_async_remote_copy(part_ref, got.at[src], send_sem.at[0], recv_sem.at[src], device_id={'pp': stage, 'tp': rank}, device_id_type=MESH)

    def greet(to_stage, offs):
        for off in offs:
            pl.semaphore_signal(bar, inc=1, device_id={'pp': to_stage, 'tp': lax.rem(rank + off, tps)}, device_id_type=MESH)

    def total(row):
        return functools.reduce(jnp.add, [got[r, row:row + 1, :] for r in range(tps)])

    @pl.when(stage != last)
    def _():
        greet(stage, range(1, tps))

        @pl.when(stage == helper)
        def _():
            greet(last, range(tps))
            pl.semaphore_wait(bar, 2 * tps - 1)
            for off in range(tps):
                copy_to(last, off, tps + off).start()

        @pl.when(stage != helper)
        def _():
            pl.semaphore_wait(bar, tps - 1)
        for off in range(1, tps):
            copy_to(stage, off, off).start()
        got[rank] = part_ref[...]
        for off in range(1, tps):
            arrived(lax.rem(rank + off, tps)).wait_recv()
        out_ref[0:1, :] = total(0)
        out_ref[1:2, :] = total(1)
        out_ref[2:3, :] = jnp.zeros((1, LANES), F)
        for off in range(1, tps):
            copy_to(stage, off, off).wait_send()

        @pl.when(stage == helper)
        def _():
            for off in range(tps):
                copy_to(last, off, tps + off).wait_send()

    @pl.when(stage == last)
    def _():
        greet(helper, range(tps))
        pl.semaphore_wait(bar, tps)
        for r in range(tps):
            arrived(r).wait_recv()
        out_ref[0:1, :] = total(2)
        out_ref[1:2, :] = total(3)
        loss = jnp.sum(total(4), axis=1, keepdims=True) * (-1.0 / toks)
        out_ref[2:3, :] = jnp.broadcast_to(loss, (1, LANES))


def solution(mesh):
    stages, tps = mesh.shape['pp'], mesh.shape['tp']
    lead = ('dp', 'pp')
    hbm = pl.BlockSpec(memory_space=pl.ANY)
    vmem = pl.BlockSpec(memory_space=pltpu.VMEM)
    S = jax.ShapeDtypeStruct

    def body(tok_ids, hid_in, cot_in, ln_gamma, ln_beta, emb_table, w_in, b_in, w_out):
        dim = hid_in.shape[-1]
        hid = hid_in.reshape(-1, dim)
        cot = cot_in.reshape(-1, dim)
        toks = hid.shape[0]
        ids = tok_ids.reshape(toks // LANES, LANES)
        table = emb_table[0]
        vocab = table.shape[0]
        ff = w_in.shape[2]
        cfg = (stages, tps, toks, dim, vocab)
        rows = toks + 2 * (toks // LANES)
        y, lab, lse, dx, did, xh, part = pl.pallas_call(
            functools.partial(stats_kernel, cfg), name='stats',
            out_shape=(S((toks, dim), B), S((8, LANES), jnp.int32), S((8, LANES), F), S((toks, dim), B), S((8, LANES), jnp.int32), S((toks, dim), F), S((8, LANES), F)),
            in_specs=[vmem] * 5 + [hbm], out_specs=[vmem] * 7,
            scratch_shapes=[
                pltpu.VMEM((vocab, dim), B), pltpu.VMEM((dim, toks), B), pltpu.VMEM((2, TILE, toks), F),
                pltpu.VMEM((rows, dim), F), pltpu.VMEM((rows, dim), F), pltpu.VMEM((rows, dim), F), pltpu.VMEM((rows, dim), F),
                pltpu.VMEM((8, LANES), F), pltpu.VMEM((tps, 8, LANES), F), pltpu.VMEM((dim, toks), F),
                pltpu.SemaphoreType.DMA, pltpu.SemaphoreType.DMA((2 + 3 * tps,)), pltpu.SemaphoreType.DMA, pltpu.SemaphoreType.DMA, pltpu.SemaphoreType.DMA((tps,))],
            compiler_params=pltpu.CompilerParams(collective_id=0, has_side_effects=True, vmem_limit_bytes=40 << 20),
        )(ids, hid, cot, ln_gamma, ln_beta, table)
        groups = (vocab // TILE - 1) // 8 + 1
        emb_grad, w1g, b1g, w2g, part = pl.pallas_call(
            functools.partial(grad_kernel, cfg), name='grads',
            out_shape=(S((vocab, dim), F), S((dim, ff), F), S((1, ff), F), S((ff, dim), F), S((8, LANES), F)),
            in_specs=[hbm] + [vmem] * 14, out_specs=[hbm] + [vmem] * 4,
            scratch_shapes=[
                pltpu.VMEM((vocab, dim), B), pltpu.VMEM((2 * dim, toks), B), pltpu.VMEM((vocab, dim), F), pltpu.VMEM((dim, toks), F),
                pltpu.SemaphoreType.DMA, pltpu.SemaphoreType.DMA((groups,))],
            compiler_params=pltpu.CompilerParams(vmem_limit_bytes=48 << 20),
        )(table, y, lab, lse, dx, did, xh, part, hid, cot, ln_gamma, ln_beta, w_in[0], b_in, w_out[0])
        sums = pl.pallas_call(
            functools.partial(sum_kernel, cfg), name='sums',
            out_shape=S((8, LANES), F), in_specs=[vmem], out_specs=vmem,
            scratch_shapes=[pltpu.VMEM((tps, 8, LANES), F), pltpu.SemaphoreType.DMA((2 * tps,)), pltpu.SemaphoreType.DMA((tps,))],
            compiler_params=pltpu.CompilerParams(collective_id=1, has_side_effects=True),
        )(part)
        return emb_grad[None], sums[2, 0:1], sums[0:1], sums[1:2], w1g[None], b1g, w2g[None]

    specs_in = (P(lead, None, None), P(lead, None, None, None), P(lead, None, None, None), P(lead, None), P(lead, None), P(lead, 'tp', None), P(lead, None, 'tp'), P(lead, 'tp'), P(lead, 'tp', None))
    specs_out = (P(lead, 'tp', None), P(lead), P(lead, None), P(lead, None), P(lead, None, 'tp'), P(lead, 'tp'), P(lead, 'tp', None))
    return jax.shard_map(body, mesh=mesh, in_specs=specs_in, out_specs=specs_out, check_vma=False)
```

time: 204 us -> 55.7 us (0.27)
  waiting for transfers between devices: 86.9 us -> 0 us
  Pallas kernels: 0 us -> 38.5 us
  other arithmetic: 36.6 us -> 0 us
  blocking collectives: 19 us -> 0 us
  matrix products: 14.7 us -> 0 us
  between operations: 15.3 us -> 0.69 us
  local copies, waits for them, and re-layouts: 27.3 us -> 15.9 us
    psum x2 -> x0, waiting for transfers between devices: 50 us -> none  [the longest x1 33.5 us: body(): d_sum = lax.psum(d_part, 'tp')]
    pallas_call x0 -> x3, Pallas kernels: none -> 38.5 us  [the longest x1 15.1 us: body(): pl.pallas_call(functools.partial(grad_kernel, cfg), name='grads', out_sha...]
    ppermute x1 -> x0, waiting for transfers between devices: 36.8 us -> none  [body(): recv_grad = lax.ppermute(tab_grad, 'pp', end_pairs)]
    another operation x5 -> x0, local copies, waits for them, and re-layouts: 26.3 us -> none
    all_gather x1 -> x0, blocking collectives: 19 us -> none  [body(): stats_all = lax.all_gather(row_stats, 'tp')]
    dot_general x3 -> x0, matrix products: 14.7 us -> none  [the longest x1 5.69 us: last_head(): lax.dot_general(norm_last, vocab_tab, CONTRACT_LAST, preferred_element_ty...]
    convert_element_type x2 -> x0, other arithmetic: 14.1 us -> none  [the longest x1 12.2 us: last_backward(): (exp_local * prob_scale - label_hit.astype(jnp.float32)).astype(jnp.bfloa...]
    reduce_sum x7 -> x0, other arithmetic: 13.4 us -> none  [the longest x1 9.46 us: last_head(): jnp.sum(exp_vals, axis=-1, keepdims=True)]
  transfers between devices with their start and end apart: 3 -> 0, of which waited for: 3 -> 0; matrix products, arithmetic and copies ran while one was open for 1% -> 0% of each run, Pallas kernels for 0% -> 0%
where the time goes in v1:
time: 55.7 us; the launch traced here: 55.1 us
  Pallas kernels  38.5 us (69%)
  local copies, waits for them, and re-layouts  15.9 us (29%)
  between operations  0.69 us (1%)
    pallas_call x1, Pallas kernels, body(): pl.pallas_call(functools.partial(grad_kernel, cfg), name='grads', out_sha...  15.1 us
    unnamed x30, local copies, waits for them, and re-layouts  13.5 us
    pallas_call x1, Pallas kernels, body(): pl.pallas_call(functools.partial(stats_kernel, cfg), name='stats', out_sh...  12.4 us
    pallas_call x1, Pallas kernels, body(): pl.pallas_call(functools.partial(sum_kernel, cfg), name='sums', out_shape...  11 us
    slice x1, local copies, waits for them, and re-layouts, body(): sums[1:2]  1.27 us
    slice x1, local copies, waits for them, and re-layouts, body(): sums[2, 0:1]  1.19 us

profile of v1, /device:TPU:7, one launch (start us, length us, event | category | flops | bytes accessed | tf_op | source)
XLA Modules:
  0.0 55.1 jit_solution(11793848719631566179)
XLA Ops:
  0.6 0.0 copy-start
  0.6 1.9 %copy-done = bf16[1,12576,128]{2,1,0:T(8,128)(2,1)S(1)} copy-done((bf16[1,12576,128]{2,1,0:T(8,128)(2,1)S(1)}, bf16[1,12576,128]{2,1,0:T(8,128)(2,1)}, u32[]{:S(2)}) %copy-start) | copy-done | bytes 3219480
  2.5 0.0 copy-start.2
  2.5 0.9 %copy-done.2 = bf16[1,1,512,128]{3,2,1,0:T(8,128)(2,1)S(1)} copy-done((bf16[1,1,512,128]{3,2,1,0:T(8,128)(2,1)S(1)}, bf16[1,1,512,128]{3,2,1,0:T(8,128)(2,1)}, u32[]{:S(2)}) %copy-start.2) | copy-done | bytes 131096
  3.4 0.0 copy-start.4
  3.5 0.9 %copy-done.4 = bf16[1,1,512,128]{3,2,1,0:T(8,128)(2,1)S(1)} copy-done((bf16[1,1,512,128]{3,2,1,0:T(8,128)(2,1)S(1)}, bf16[1,1,512,128]{3,2,1,0:T(8,128)(2,1)}, u32[]{:S(2)}) %copy-start.4) | copy-done | bytes 131096
  4.4 0.0 copy-start.9
  4.4 0.7 %copy-done.9 = s32[1,1,512]{2,1,0:T(1,128)S(1)} copy-done((s32[1,1,512]{2,1,0:T(1,128)S(1)}, s32[1,1,512]{2,1,0:T(1,128)}, u32[]{:S(2)}) %copy-start.9) | copy-done | bytes 2072
  5.0 0.0 copy-start.10
  5.0 0.7 %copy-done.10 = f32[1,128]{1,0:T(1,128)S(1)} copy-done((f32[1,128]{1,0:T(1,128)S(1)}, f32[1,128]{1,0:T(1,128)}, u32[]{:S(2)}) %copy-start.10) | copy-done | bytes 536
  5.7 0.0 copy-start.12
  5.7 0.7 %copy-done.12 = f32[1,128]{1,0:T(1,128)S(1)} copy-done((f32[1,128]{1,0:T(1,128)S(1)}, f32[1,128]{1,0:T(1,128)}, u32[]{:S(2)}) %copy-start.12) | copy-done | bytes 536
  6.3 12.4 %stats.1 = (bf16[512,128]{1,0:T(8,128)(2,1)S(1)}, s32[8,128]{1,0:T(8,128)S(1)}, f32[8,128]{1,0:T(8,128)S(1)}, bf16[512,128]{1,0:T(8,128)(2,1)S(1)}, s32[8,128]{1...) custom-call(s32[4,128]{1,0:T(4,128)S(1)} %bitcast.18, bf16[512,128]{1,0:T(8,128)(2,1)S(1)} %bitcast.12, ...), custom_call_target="tpu_custom_call" | custom-call | tf_op jit(solution)/shard_map/stats/pallas_call | solution.py:427
  18.7 0.0 copy-start.1
  18.7 1.9 %copy-done.1 = bf16[1,12576,128]{2,1,0:T(8,128)(2,1)S(1)} copy-done((bf16[1,12576,128]{2,1,0:T(8,128)(2,1)S(1)}, bf16[1,12576,128]{2,1,0:T(8,128)(2,1)}, u32[]{:S(2)}) %copy-start.1) | copy-done | bytes 3219480
  20.6 0.0 copy-start.3
  20.6 0.9 %copy-done.3 = bf16[1,1,512,128]{3,2,1,0:T(8,128)(2,1)S(1)} copy-done((bf16[1,1,512,128]{3,2,1,0:T(8,128)(2,1)S(1)}, bf16[1,1,512,128]{3,2,1,0:T(8,128)(2,1)}, u32[]{:S(2)}) %copy-start.3) | copy-done | bytes 131096
  21.5 0.0 copy-start.5
  21.5 0.9 %copy-done.5 = bf16[1,1,512,128]{3,2,1,0:T(8,128)(2,1)S(1)} copy-done((bf16[1,1,512,128]{3,2,1,0:T(8,128)(2,1)S(1)}, bf16[1,1,512,128]{3,2,1,0:T(8,128)(2,1)}, u32[]{:S(2)}) %copy-start.5) | copy-done | bytes 131096
  22.4 0.0 copy-start.6
  22.4 0.8 %copy-done.6 = bf16[1,128,128]{2,1,0:T(8,128)(2,1)S(1)} copy-done((bf16[1,128,128]{2,1,0:T(8,128)(2,1)S(1)}, bf16[1,128,128]{2,1,0:T(8,128)(2,1)}, u32[]{:S(2)}) %copy-start.6) | copy-done | bytes 32792
  23.2 0.0 copy-start.7
  23.2 0.8 %copy-done.7 = bf16[1,128,128]{2,1,0:T(8,128)(2,1)S(1)} copy-done((bf16[1,128,128]{2,1,0:T(8,128)(2,1)S(1)}, bf16[1,128,128]{2,1,0:T(8,128)(2,1)}, u32[]{:S(2)}) %copy-start.7) | copy-done | bytes 32792
  24.0 0.7 %copy-done.11 = f32[1,128]{1,0:T(1,128)S(1)} copy-done((f32[1,128]{1,0:T(1,128)S(1)}, f32[1,128]{1,0:T(1,128)}, u32[]{:S(2)}) %copy-start.11) | copy-done | bytes 536
  24.6 0.7 %copy-done.13 = f32[1,128]{1,0:T(1,128)S(1)} copy-done((f32[1,128]{1,0:T(1,128)S(1)}, f32[1,128]{1,0:T(1,128)}, u32[]{:S(2)}) %copy-start.13) | copy-done | bytes 536
  25.3 0.7 %copy-done.14 = f32[1,128]{1,0:T(1,128)S(1)} copy-done((f32[1,128]{1,0:T(1,128)S(1)}, f32[1,128]{1,0:T(1,128)}, u32[]{:S(2)}) %copy-start.14) | copy-done | bytes 536
  25.9 15.1 %grads.1 = (f32[12576,128]{1,0:T(8,128)}, f32[128,128]{1,0:T(8,128)}, f32[1,128]{1,0:T(1,128)}, f32[128,128]{1,0:T(8,128)}, f32[8,128]{1,0:T(8,128)S(1)}) custom-call(bf16[12576,128]{1,0:T(8,128)(2,1)S(1)} %bitcast.11, bf16[512,128]{1,0:T(8,128)(2,1)S(1)} %get-tuple-element.19.y_ref, s32[8,128]{1,0:T(8,128)S(1)} %get-tuple-element.20.lab_ref, ...), custom_call_target="tpu_custom_call" | custom-call | tf_op jit(solution)/shard_map/grads/pallas_call | solution.py:439
  41.0 0.0 copy-start.8
  41.0 0.6 %copy-done.8 = f32[8,128]{1,0:T(8,128)} copy-done((f32[8,128]{1,0:T(8,128)}, f32[8,128]{1,0:T(8,128)S(1)}, u32[]{:S(2)}) %copy-start.8) | copy-done | bytes 4120
  41.6 11.0 %sums.1 = f32[8,128]{1,0:T(8,128)} custom-call(f32[8,128]{1,0:T(8,128)} %copy-done.8), custom_call_target="tpu_custom_call" | custom-call | tf_op jit(solution)/shard_map/sums/pallas_call | solution.py:448
  52.6 1.2 %slice.9 = f32[1,1]{1,0:T(1,128)} slice(f32[8,128]{1,0:T(8,128)} %sums.1), slice={[2:3], [0:1]} | slice | bytes 8 | tf_op jit(solution)/shard_map/slice | solution.py:454
  53.8 1.3 %fusion = (f32[1,128]{1,0:T(1,128)}, f32[1,128]{1,0:T(1,128)}) fusion(f32[8,128]{1,0:T(8,128)} %sums.1), kind=kLoop, calls=%fused_computation | loop fusion | bytes 2048 | tf_op jit(solution)/shard_map/slice | solution.py:454
  (3 shorter events, 0.0 us)
Async XLA Ops:
  0.6 1.9 %copy-start = (bf16[1,12576,128]{2,1,0:T(8,128)(2,1)S(1)}, bf16[1,12576,128]{2,1,0:T(8,128)(2,1)}, u32[]{:S(2)}) copy-start(bf16[1,12576,128]{2,1,0:T(8,128)(2,1)} %param.14) | copy-start | bytes 9658372
  2.5 0.9 %copy-start.2 = (bf16[1,1,512,128]{3,2,1,0:T(8,128)(2,1)S(1)}, bf16[1,1,512,128]{3,2,1,0:T(8,128)(2,1)}, u32[]{:S(2)}) copy-start(bf16[1,1,512,128]{3,2,1,0:T(8,128)(2,1)} %param.10) | copy-start | bytes 393220
  3.4 0.9 %copy-start.4 = (bf16[1,1,512,128]{3,2,1,0:T(8,128)(2,1)S(1)}, bf16[1,1,512,128]{3,2,1,0:T(8,128)(2,1)}, u32[]{:S(2)}) copy-start(bf16[1,1,512,128]{3,2,1,0:T(8,128)(2,1)} %param.11) | copy-start | bytes 393220
  4.4 0.7 %copy-start.9 = (s32[1,1,512]{2,1,0:T(1,128)S(1)}, s32[1,1,512]{2,1,0:T(1,128)}, u32[]{:S(2)}) copy-start(s32[1,1,512]{2,1,0:T(1,128)} %param.9) | copy-start | bytes 6148
  5.0 0.7 %copy-start.10 = (f32[1,128]{1,0:T(1,128)S(1)}, f32[1,128]{1,0:T(1,128)}, u32[]{:S(2)}) copy-start(f32[1,128]{1,0:T(1,128)} %gam_ref.3) | copy-start | bytes 1540
  5.7 0.7 %copy-start.12 = (f32[1,128]{1,0:T(1,128)S(1)}, f32[1,128]{1,0:T(1,128)}, u32[]{:S(2)}) copy-start(f32[1,128]{1,0:T(1,128)} %bet_ref.3) | copy-start | bytes 1540
  18.7 1.9 %copy-start.1 = (bf16[1,12576,128]{2,1,0:T(8,128)(2,1)S(1)}, bf16[1,12576,128]{2,1,0:T(8,128)(2,1)}, u32[]{:S(2)}) copy-start(bf16[1,12576,128]{2,1,0:T(8,128)(2,1)} %param.14) | copy-start | bytes 9658372
  20.6 0.9 %copy-start.3 = (bf16[1,1,512,128]{3,2,1,0:T(8,128)(2,1)S(1)}, bf16[1,1,512,128]{3,2,1,0:T(8,128)(2,1)}, u32[]{:S(2)}) copy-start(bf16[1,1,512,128]{3,2,1,0:T(8,128)(2,1)} %param.10) | copy-start | bytes 393220
  21.5 0.9 %copy-start.5 = (bf16[1,1,512,128]{3,2,1,0:T(8,128)(2,1)S(1)}, bf16[1,1,512,128]{3,2,1,0:T(8,128)(2,1)}, u32[]{:S(2)}) copy-start(bf16[1,1,512,128]{3,2,1,0:T(8,128)(2,1)} %param.11) | copy-start | bytes 393220
  22.4 0.8 %copy-start.6 = (bf16[1,128,128]{2,1,0:T(8,128)(2,1)S(1)}, bf16[1,128,128]{2,1,0:T(8,128)(2,1)}, u32[]{:S(2)}) copy-start(bf16[1,128,128]{2,1,0:T(8,128)(2,1)} %param.15) | copy-start | bytes 98308
  23.2 0.8 %copy-start.7 = (bf16[1,128,128]{2,1,0:T(8,128)(2,1)S(1)}, bf16[1,128,128]{2,1,0:T(8,128)(2,1)}, u32[]{:S(2)}) copy-start(bf16[1,128,128]{2,1,0:T(8,128)(2,1)} %param.17) | copy-start | bytes 98308
  24.0 0.7 %copy-start.11 = (f32[1,128]{1,0:T(1,128)S(1)}, f32[1,128]{1,0:T(1,128)}, u32[]{:S(2)}) copy-start(f32[1,128]{1,0:T(1,128)} %gam_ref.3) | copy-start | bytes 1540
  24.6 0.7 %copy-start.13 = (f32[1,128]{1,0:T(1,128)S(1)}, f32[1,128]{1,0:T(1,128)}, u32[]{:S(2)}) copy-start(f32[1,128]{1,0:T(1,128)} %bet_ref.3) | copy-start | bytes 1540
  25.3 0.7 %copy-start.14 = (f32[1,128]{1,0:T(1,128)S(1)}, f32[1,128]{1,0:T(1,128)}, u32[]{:S(2)}) copy-start(f32[1,128]{1,0:T(1,128)} %b1_ref.1) | copy-start | bytes 1540
  41.0 0.6 %copy-start.8 = (f32[8,128]{1,0:T(8,128)}, f32[8,128]{1,0:T(8,128)S(1)}, u32[]{:S(2)}) copy-start(f32[8,128]{1,0:T(8,128)S(1)} %get-tuple-element.27.part_ref) | copy-start | bytes 12292

commit v2 on v0

v2 whole, which is shorter than its diff:
```python
import functools

import jax
import jax.numpy as jnp
from jax import lax
from jax.experimental import pallas as pl
from jax.experimental.pallas import tpu as pltpu
from jax.sharding import PartitionSpec as P

F = jnp.float32
B = jnp.bfloat16
LN_EPS = 1e-5
LOG2E = 1.4426950408889634
LANES = 128
TILE = 256
SPLIT_STATS = 34
SPLIT_DY = 26
EARLY = 8
GRANT = 20 << 20
MESH = pl.DeviceIdType.MESH
NT = (((1,), (1,)), ((), ()))
TN = (((0,), (0,)), ((), ()))


def ln_hat(rows):
    centre = rows - jnp.mean(rows, axis=-1, keepdims=True)
    inv = lax.rsqrt(jnp.mean(centre * centre, axis=-1, keepdims=True) + LN_EPS)
    return centre * inv, inv


def mm(a, b):
    return jnp.dot(a, b, preferred_element_type=F)


def lanes_row(ref, first, chunks):
    return jnp.concatenate([ref[first + c:first + c + 1, :] for c in range(chunks)], axis=1)


def stats_kernel(cfg, ids_hbm, hid_hbm, cot_hbm, gam_hbm, bet_hbm, emb_hbm, w1_hbm, b1_hbm, w2_hbm,
                 e_ref, log_ref, y_out, lab_out, lse_out, dx_out, did_out, xh_out, part_out, w1_out, b1_out, w2_out,
                 ids_ref, hid_ref, cot_ref, gam_ref, bet_ref, w1_ref, b1_ref, w2_ref, ids_smem,
                 yt_ref, pack_src, pack_dst, dx_src, dx_dst, st_src, st_all, e32_ref, x_ref, part_src, part_all,
                 e_sem, in_sem, send_sem, pack_sem, dx_sem, st_sem, part_sem):
    stages, tps, toks, dim, vocab = cfg
    chunks = toks // LANES
    rank = lax.axis_index('tp')
    stage = lax.axis_index('pp')
    last = stages - 1
    helper = stages - 2
    full, tail = vocab // TILE - 1, vocab - (vocab // TILE - 1) * TILE
    e_copy = pltpu.make_async_copy(emb_hbm, e_ref, e_sem)
    pairs = ((hid_hbm, hid_ref), (ids_hbm, ids_ref), (gam_hbm, gam_ref), (bet_hbm, bet_ref), (cot_hbm, cot_ref), (ids_hbm, ids_smem), (w1_hbm, w1_ref), (b1_hbm, b1_ref), (w2_hbm, w2_ref))
    hid_ld, ids_ld, gam_ld, bet_ld, cot_ld, smem_ld, w1_ld, b1_ld, w2_ld = [pltpu.make_async_copy(a, b, in_sem.at[i]) for i, (a, b) in enumerate(pairs)]

    def fetch(*copies):
        for copy in copies:
            copy.start()

    def ready(*copies):
        for copy in copies:
            copy.wait()

    def remote(src, dst, ssem, rsem, to_stage, off=0):
        return pltpu.make_async_remote_copy(src, dst, ssem, rsem, device_id={'pp': to_stage, 'tp': lax.rem(rank + off, tps)}, device_id_type=MESH)

    def pack_copy(to_stage, idx, src=None):
        return remote(pack_src if src is None else src, pack_dst, send_sem.at[idx], pack_sem, to_stage)

    def dx_copy():
        return remote(dx_src, dx_dst, send_sem.at[0], dx_sem, last)

    def part_copy(off):
        return remote(part_src, part_all.at[rank], send_sem.at[off], part_sem.at[rank], 0, off)

    def greet():
        bar = pltpu.get_barrier_semaphore()
        for ds in range(stages):
            for off in range(tps):
                if ds or off:
                    pl.semaphore_signal(bar, inc=1, device_id={'pp': lax.rem(stage + ds, stages), 'tp': lax.rem(rank + off, tps)}, device_id_type=MESH)

    def met():
        pl.semaphore_wait(pltpu.get_barrier_semaphore(), stages * tps - 1)

    def normed(rows, gam, bet):
        hat, _ = ln_hat(rows)
        norm = (hat * gam + bet).astype(B)
        xh_out[...] = hat
        y_out[...] = norm
        yt_ref[...] = norm.astype(F).T.astype(B)

    def unpack():
        normed(pack_dst[0:toks, :], pack_dst[toks + chunks:toks + chunks + 1, :], pack_dst[toks + chunks + 1:toks + chunks + 2, :])
        lab_out[0:chunks, :] = pack_dst[toks:toks + chunks, :].astype(jnp.int32)

    def st_sends(which):
        slot = 2 * rank + which
        return [remote(st_src, st_all.at[slot], send_sem.at[2 + i], st_sem.at[slot], lax.rem(stage + ds, stages), off) for i, (ds, off) in enumerate((ds, off) for ds in range(stages) for off in range(tps) if ds or off)]

    def st_wait(slot):
        remote(st_src, st_all.at[slot], send_sem.at[0], st_sem.at[slot], last).wait_recv()

    def finish_stats():
        tops = [st_all[r, 0:chunks, :] for r in range(2 * tps)]
        sums = [st_all[r, chunks:2 * chunks, :] for r in range(2 * tps)]
        top = functools.reduce(jnp.maximum, tops)
        tot = functools.reduce(jnp.add, [s * jnp.exp(t - top) for s, t in zip(sums, tops)])
        lse_out[0:chunks, :] = top + jnp.log(tot)

    def logit_tile(row, size):
        logits = mm(e_ref[pl.ds(row, size), :], yt_ref[...])
        log_ref[pl.ds(row, size), :] = logits
        return logits

    def fill_logits(first, end):
        def step(i, carry):
            logit_tile(pl.multiple_of(i * TILE, TILE), TILE)
            return carry
        lax.fori_loop(first, end, step, 0, unroll=min(8, end - first))

    def logits_to(row, top, size=TILE):
        return jnp.maximum(top, jnp.max(logit_tile(row, size).reshape(size // 8, 8, toks), axis=0))

    def add_exp(row, top_old, top, tot, size=TILE):
        ex = jnp.exp(log_ref[pl.ds(row, size), :].reshape(size // 8, 8, toks) - top[None])
        return tot * jnp.exp(top_old - top) + jnp.sum(ex, axis=0)

    def begin_stats(first):
        low = jnp.full((8, toks), -jnp.inf, F)
        top = logits_to(first * TILE, low)
        return top, top, jnp.zeros((8, toks), F)

    def run_stats(first, end, carry):
        def step(i, carry):
            old, top, tot = carry
            row = pl.multiple_of(i * TILE, TILE)
            new = logits_to(row + TILE, top)
            return top, new, add_exp(row, old, top, tot)
        return lax.fori_loop(first, end, step, carry, unroll=min(8, end - first))

    def share_stats(top, tot, which):
        high = jnp.max(top, axis=0, keepdims=True)
        tot = jnp.sum(tot * jnp.exp(top - high), axis=0, keepdims=True)
        for c in range(chunks):
            st_src[c:c + 1, :] = high[:, c * LANES:(c + 1) * LANES]
            st_src[chunks + c:chunks + c + 1, :] = tot[:, c * LANES:(c + 1) * LANES]
        st_all[2 * rank + which] = st_src[...]
        sends = st_sends(which)
        for send in sends:
            send.start()
        return sends

    def mlp():
        ready(hid_ld, cot_ld, gam_ld, bet_ld, w1_ld, b1_ld, w2_ld)
        hat, _ = ln_hat(hid_ref[...].astype(F))
        norm = (hat * gam_ref[...] + bet_ref[...]).astype(B)
        pre = mm(norm, w1_ref[...]) + b1_ref[...]
        cube = 0.7978845608028654 * (pre + 0.044715 * (pre * pre * pre))
        th = jnp.tanh(cube)
        act = pre * (0.5 * (1.0 + th))
        slope = 0.5 * (1.0 + th) + pre * (0.5 * (1.0 - th * th)) * (0.7978845608028654 * (1.0 + 3 * 0.044715 * pre * pre))
        w2_out[...] = lax.dot_general(act.astype(B), cot_ref[...], TN, preferred_element_type=F)
        d_act = lax.dot_general(cot_ref[...], w2_ref[...], NT, preferred_element_type=F)
        d_pre = d_act * slope
        d_b = d_pre.astype(B)
        w1_out[...] = lax.dot_general(norm, d_b, TN, preferred_element_type=F)
        b1_out[...] = jnp.sum(d_pre, axis=0, keepdims=True)
        d_h = lax.dot_general(d_b, w1_ref[...], NT, preferred_element_type=F)
        part_out[0:1, :] = jnp.sum(d_h * hat, axis=0, keepdims=True)
        part_out[1:2, :] = jnp.sum(d_h, axis=0, keepdims=True)
        part_out[2:8, :] = jnp.zeros((6, LANES), F)

    @pl.when(stage == last)
    def _():
        fetch(hid_ld, ids_ld, gam_ld, bet_ld, e_copy)
        greet()
        ready(hid_ld, ids_ld, gam_ld, bet_ld)
        rows = hid_ref[...].astype(F)
        pack_src[0:toks, :] = rows
        pack_src[toks:toks + chunks, :] = ids_ref[...].astype(F)
        pack_src[toks + chunks:toks + chunks + 1, :] = gam_ref[...]
        pack_src[toks + chunks + 1:toks + chunks + 2, :] = bet_ref[...]
        normed(rows, gam_ref[...], bet_ref[...])
        lab_out[0:chunks, :] = ids_ref[...]
        e_copy.wait()
        carry = run_stats(0, EARLY, begin_stats(0))
        met()
        pack_copy(helper, 1).start()
        pack_copy(0, 0).start()
        old, top, tot = run_stats(EARLY, SPLIT_STATS - 1, carry)
        tot = add_exp((SPLIT_STATS - 1) * TILE, old, top, tot)
        sends = share_stats(top, tot, 0)
        fill_logits(SPLIT_STATS, full)
        logit_tile(full * TILE, tail)
        dx_copy().wait_recv()
        dx_out[...] = dx_dst[0:toks, :].astype(B)
        did_out[0:chunks, :] = dx_dst[toks:toks + chunks, :].astype(jnp.int32)
        st_wait(2 * rank + 1)
        for off in range(1, tps):
            st_wait(2 * lax.rem(rank + off, tps))
            st_wait(2 * lax.rem(rank + off, tps) + 1)
        finish_stats()
        pack_copy(helper, 1).wait_send()
        pack_copy(0, 0).wait_send()
        for send in sends:
            send.wait_send()

    @pl.when(stage == helper)
    def _():
        fetch(hid_ld, cot_ld, gam_ld, bet_ld, w1_ld, b1_ld, w2_ld, e_copy)
        greet()
        mlp()
        met()
        e_copy.wait()
        pack_copy(helper, 1).wait_recv()
        unpack()
        old, top, tot = run_stats(SPLIT_STATS, full - 1, begin_stats(SPLIT_STATS))
        new = logits_to(full * TILE, top, tail)
        tot = add_exp((full - 1) * TILE, old, top, tot)
        tot = add_exp(full * TILE, top, new, tot, tail)
        sends = share_stats(new, tot, 1)
        fill_logits(SPLIT_DY, SPLIT_STATS)
        st_wait(2 * rank)
        for off in range(1, tps):
            st_wait(2 * lax.rem(rank + off, tps))
            st_wait(2 * lax.rem(rank + off, tps) + 1)
        finish_stats()
        for send in sends:
            send.wait_send()

    @pl.when(stage == 0)
    def _():
        fetch(cot_ld, ids_ld, gam_ld, smem_ld, e_copy)
        greet()
        ready(cot_ld, ids_ld, gam_ld, smem_ld)
        e_copy.wait()

        def widen(i, carry):
            row = pl.multiple_of(i * TILE, TILE)
            e32_ref[pl.ds(row, TILE), :] = e_ref[pl.ds(row, TILE), :].astype(F)
            return carry

        lax.fori_loop(0, full, widen, 0, unroll=4)
        e32_ref[full * TILE:vocab, :] = e_ref[full * TILE:vocab, :].astype(F)
        base = rank * vocab
        for c in range(chunks):
            def pick(i, carry):
                row = jnp.clip(ids_smem[c, i] - base, 0, vocab - 1)
                x_ref[pl.ds(c * LANES + i, 1), :] = e32_ref[pl.ds(row, 1), :]
                return carry
            lax.fori_loop(0, LANES, pick, 0, unroll=16)
        local = lanes_row(ids_ref, 0, chunks) - base
        inside = jnp.where((local >= 0) & (local < vocab), 1.0, 0.0)
        mask = jnp.broadcast_to(inside, (LANES, toks)).T
        hat, inv = ln_hat(x_ref[...])
        cot = cot_ref[...].astype(F)
        scaled = cot * gam_ref[...]
        grad = inv * (scaled - jnp.mean(scaled, axis=-1, keepdims=True) - hat * jnp.mean(scaled * hat, axis=-1, keepdims=True))
        grad = jnp.where(mask > 0.5, grad, 0.0).astype(B)
        dx_out[...] = grad
        did_out[0:chunks, :] = ids_ref[...]
        dx_src[0:toks, :] = grad.astype(F)
        dx_src[toks:toks + chunks, :] = ids_ref[...].astype(F)
        part_src[0:1, :] = jnp.sum(jnp.where(mask > 0.5, cot * hat, 0.0), axis=0, keepdims=True)
        part_src[1:2, :] = jnp.sum(jnp.where(mask > 0.5, cot, 0.0), axis=0, keepdims=True)
        part_src[2:8, :] = jnp.zeros((6, LANES), F)
        part_all[rank] = part_src[...]
        met()
        dx_copy().start()
        for off in range(1, tps):
            part_copy(off).start()
        pack_copy(0, 0).wait_recv()
        pack_copy(1, 2 + tps, pack_dst).start()
        unpack()
        fill_logits(0, full)
        logit_tile(full * TILE, tail)
        for off in range(1, tps):
            src = lax.rem(rank + off, tps)
            remote(part_src, part_all.at[src], send_sem.at[0], part_sem.at[src], 0).wait_recv()
        part_out[...] = functools.reduce(jnp.add, [part_all[r] for r in range(tps)])
        for slot in range(2 * tps):
            st_wait(slot)
        finish_stats()
        dx_copy().wait_send()
        pack_copy(1, 2 + tps, pack_dst).wait_send()
        for off in range(1, tps):
            part_copy(off).wait_send()

    @pl.when((stage != 0) & (stage != helper) & (stage != last))
    def _():
        fetch(hid_ld, cot_ld, gam_ld, bet_ld, w1_ld, b1_ld, w2_ld, e_copy)
        greet()
        mlp()
        met()
        e_copy.wait()
        pack_copy(0, 0).wait_recv()
        unpack()
        fill_logits(0, SPLIT_DY)
        for slot in range(2 * tps):
            st_wait(slot)
        finish_stats()


def grad_kernel(cfg, e_ref, log_ref, y_ref, lab_ref, lse_ref, dx_ref, did_ref, xh_ref, pin_ref, w1_in, b1_in, w2_in,
                emb_out, w1_out, b1_out, w2_out, part_out, out_ref, dyt_ref, o_sem):
    stages, tps, toks, dim, vocab = cfg
    chunks = toks // LANES
    rank = lax.axis_index('tp')
    stage = lax.axis_index('pp')
    last = stages - 1
    helper = stages - 2
    base = rank * vocab
    full, tail = vocab // TILE - 1, vocab - (vocab // TILE - 1) * TILE
    group = 16
    groups = full // group
    size16 = group * TILE

    @pl.when((stage == 0) | (stage == last))
    def _():
        w1_out[...] = jnp.zeros(w1_out.shape, F)
        b1_out[...] = jnp.zeros(b1_out.shape, F)
        w2_out[...] = jnp.zeros(w2_out.shape, F)
        part_out[...] = pin_ref[...]
        lse = lanes_row(lse_ref, 0, chunks)
        lab = (lanes_row(lab_ref, 0, chunks) - base)
        did = (lanes_row(did_ref, 0, chunks) - base)
        lab = jnp.where((lab >= 0) & (lab < vocab), lab, -1).astype(jnp.int16)
        did = jnp.where((did >= 0) & (did < vocab), did, -1).astype(jnp.int16)

        def out_copy(c):
            size = tail if c == groups else size16
            return pltpu.make_async_copy(out_ref.at[pl.ds(c * size16, size)], emb_out.at[pl.ds(c * size16, size)], o_sem.at[c])

        def work(row, size):
            p = jnp.exp2((log_ref[pl.ds(row, size), :] - lse) * LOG2E)
            rows = (lax.broadcasted_iota(jnp.int32, (size, LANES), 0) + row).astype(jnp.int16)
            one, zero = jnp.ones((size, LANES), B), jnp.zeros((size, LANES), B)
            g, h = [], []
            for c in range(chunks):
                cols = slice(c * LANES, (c + 1) * LANES)
                pc = p[:, cols]
                g.append(jnp.where(rows == lab[:, cols], (pc - 1.0).astype(B), pc.astype(B)))
                h.append(jnp.where(rows == did[:, cols], one, zero))
            out_ref[pl.ds(row, size), :] = mm(jnp.concatenate(g, axis=1), y_ref[...]) + mm(jnp.concatenate(h, axis=1), dx_ref[...])

        for c in range(groups):
            def step(i, carry):
                work(pl.multiple_of(c * size16 + i * TILE, TILE), TILE)
                return carry
            lax.fori_loop(0, group, step, 0, unroll=16)
            out_copy(c).start()
        work(full * TILE, tail)
        out_copy(groups).start()
        for c in range(groups + 1):
            out_copy(c).wait()

    @pl.when((stage != 0) & (stage != last))
    def _():
        out_ref[0:size16, :] = jnp.zeros((size16, dim), F)

        def zero_copy(c):
            n = tail if c == groups else size16
            return pltpu.make_async_copy(out_ref.at[pl.ds(0, n)], emb_out.at[pl.ds(c * size16, n)], o_sem.at[c])

        for c in range(groups + 1):
            zero_copy(c).start()
        w1_out[...] = w1_in[...]
        b1_out[...] = b1_in[...]
        w2_out[...] = w2_in[...]
        part_out[...] = pin_ref[...]
        lse = lanes_row(lse_ref, 0, chunks)
        lab = lanes_row(lab_ref, 0, chunks) - base
        dyt_ref[...] = jnp.zeros((dim, toks), F)

        def work(row, size, loss):
            x = log_ref[pl.ds(row, size), :] - lse
            p = jnp.exp2(x * LOG2E)
            rows = lax.broadcasted_iota(jnp.int32, (size, LANES), 0) + row
            g, picked = [], []
            for c in range(chunks):
                cols = slice(c * LANES, (c + 1) * LANES)
                hit = rows == lab[:, cols]
                pc = p[:, cols]
                g.append(jnp.where(hit, pc - 1.0, pc).astype(B))
                picked.append(jnp.sum(jnp.where(hit, x[:, cols], 0.0).reshape(size // 8, 8, LANES), axis=0))
            dyt_ref[...] += lax.dot_general(e_ref[pl.ds(row, size), :], jnp.concatenate(g, axis=1), TN, preferred_element_type=F)
            return loss + functools.reduce(jnp.add, picked)

        def sweep(first, end, loss):
            def step(i, loss):
                return work(pl.multiple_of(i * TILE, TILE), TILE, loss)
            return lax.fori_loop(first, end, step, loss, unroll=min(8, end - first))

        def finish(loss):
            dy = dyt_ref[...].T
            part_out[2:3, :] = jnp.sum(dy * xh_ref[...], axis=0, keepdims=True)
            part_out[3:4, :] = jnp.sum(dy, axis=0, keepdims=True)
            part_out[4:5, :] = jnp.sum(loss, axis=0, keepdims=True)

        @pl.when(stage == helper)
        def _():
            loss = sweep(SPLIT_DY, full, jnp.zeros((8, LANES), F))
            finish(work(full * TILE, tail, loss))

        @pl.when(stage != helper)
        def _():
            finish(sweep(0, SPLIT_DY, jnp.zeros((8, LANES), F)))

        for c in range(groups + 1):
            zero_copy(c).wait()


def sum_kernel(cfg, part_ref, sum_out, got, send_sem, recv_sem):
    stages, tps, toks, dim, vocab = cfg
    rank = lax.axis_index('tp')
    stage = lax.axis_index('pp')
    last = stages - 1
    helper = stages - 2
    mids = helper
    bar = pltpu.get_barrier_semaphore()

    def copy_to(to_stage, off, idx):
        slot = (stage - 1) * tps + rank
        return pltpu.make_async_remote_copy(part_ref, got.at[slot], send_sem.at[idx], recv_sem.at[slot], device_id={'pp': to_stage, 'tp': lax.rem(rank + off, tps)}, device_id_type=MESH)

    def arrived(slot):
        return pltpu.make_async_remote_copy(part_ref, got.at[slot], send_sem.at[0], recv_sem.at[slot], device_id={'tp': rank}, device_id_type=MESH)

    def total(at):
        return functools.reduce(jnp.add, [got[at * tps + r] for r in range(tps)])

    @pl.when((stage != 0) & (stage != last))
    def _():
        for to_stage in range(1, 1 + mids):
            for off in range(tps):
                @pl.when((stage != to_stage) | (off != 0))
                def _():
                    pl.semaphore_signal(bar, inc=1, device_id={'pp': to_stage, 'tp': lax.rem(rank + off, tps)}, device_id_type=MESH)
        pl.semaphore_wait(bar, mids * tps - 1)

        @pl.when(stage == helper)
        def _():
            sends = [copy_to(helper, off, off) for off in range(1, tps)]
            for send in sends:
                send.start()
            got[(helper - 1) * tps + rank] = part_ref[...]
            for at in range(helper - 1):
                for r in range(tps):
                    arrived(at * tps + r).wait_recv()
            for off in range(1, tps):
                arrived((helper - 1) * tps + lax.rem(rank + off, tps)).wait_recv()
            own = total(helper - 1)
            rest = functools.reduce(jnp.add, [total(at) for at in range(helper)])
            sum_out[...] = jnp.concatenate([own[0:2, :], rest[2:8, :]], axis=0)
            for send in sends:
                send.wait_send()

        @pl.when(stage != helper)
        def _():
            sends = [copy_to(helper, off, tps + off) for off in range(tps)] + [copy_to(stage, off, off) for off in range(1, tps)]
            for send in sends:
                send.start()
            mine = (stage - 1) * tps
            got[mine + rank] = part_ref[...]
            for off in range(1, tps):
                arrived(mine + lax.rem(rank + off, tps)).wait_recv()
            sum_out[...] = functools.reduce(jnp.add, [got[mine + r] for r in range(tps)])
            for send in sends:
                send.wait_send()

    @pl.when((stage == 0) | (stage == last))
    def _():
        sum_out[...] = part_ref[...]


def hand_kernel(cfg, sum_ref, gam_out, bet_out, loss_out, got, send_sem, recv_sem):
    stages, tps, toks, dim, vocab = cfg
    stage = lax.axis_index('pp')
    last = stages - 1
    helper = stages - 2
    bar = pltpu.get_barrier_semaphore()

    def hand_over():
        return pltpu.make_async_remote_copy(sum_ref, got, send_sem, recv_sem, device_id={'pp': last}, device_id_type=MESH)

    @pl.when(stage == helper)
    def _():
        pl.semaphore_signal(bar, inc=1, device_id={'pp': last}, device_id_type=MESH)
        pl.semaphore_wait(bar, 1)
        hand_over().start()
        hand_over().wait_send()

    @pl.when(stage != last)
    def _():
        gam_out[...] = sum_ref[0:1, :]
        bet_out[...] = sum_ref[1:2, :]
        loss_out[...] = jnp.zeros((1, 1), F)

    @pl.when(stage == last)
    def _():
        pl.semaphore_signal(bar, inc=1, device_id={'pp': helper}, device_id_type=MESH)
        pl.semaphore_wait(bar, 1)
        hand_over().wait_recv()
        gam_out[...] = got[2:3, :]
        bet_out[...] = got[3:4, :]
        loss_out[...] = jnp.sum(got[4:5, :], axis=1, keepdims=True) * (-1.0 / toks)


def solution(mesh):
    stages, tps = mesh.shape['pp'], mesh.shape['tp']
    lead = ('dp', 'pp')
    hbm = pl.BlockSpec(memory_space=pltpu.HBM)
    vmem = pl.BlockSpec(memory_space=pltpu.VMEM)
    S = jax.ShapeDtypeStruct
    V = pltpu.VMEM
    DMA = pltpu.SemaphoreType.DMA
    I = jnp.int32

    def stay(*arrays):
        return [pltpu.with_memory_space_constraint(a, pltpu.HBM) for a in arrays]

    def body(tok_ids, hid_in, cot_in, ln_gamma, ln_beta, emb_table, w_in, b_in, w_out):
        dim = hid_in.shape[-1]
        hid = hid_in.reshape(-1, dim)
        cot = cot_in.reshape(-1, dim)
        toks = hid.shape[0]
        chunks = toks // LANES
        ids = tok_ids.reshape(chunks, LANES)
        table = emb_table[0]
        vocab = table.shape[0]
        ff = w_in.shape[2]
        cfg = (stages, tps, toks, dim, vocab)
        rows = toks + 2 * chunks
        vec = S((8, LANES), F)
        weights = (S((dim, ff), F), S((1, ff), F), S((ff, dim), F))
        mids = pl.pallas_call(
            functools.partial(stats_kernel, cfg), name='stats',
            out_shape=(S((vocab, dim), B), S((vocab, toks), F), S((toks, dim), B), S((8, LANES), I), vec, S((toks, dim), B), S((8, LANES), I), S((toks, dim), F), vec) + weights,
            in_specs=[hbm] * 9, out_specs=[vmem] * 12,
            scratch_shapes=[
                V((chunks, LANES), I), V((toks, dim), B), V((toks, dim), B), V((1, dim), F), V((1, dim), F), V((dim, ff), B), V((1, ff), F), V((ff, dim), B), pltpu.SMEM((chunks, LANES), I),
                V((dim, toks), B), V((rows, dim), F), V((rows, dim), F), V((rows, dim), F), V((rows, dim), F),
                V((8, LANES), F), V((2 * tps, 8, LANES), F), V((vocab, dim), F), V((toks, dim), F), V((8, LANES), F), V((tps, 8, LANES), F),
                DMA, DMA((9,)), DMA((2 + stages * tps,)), DMA, DMA, DMA((2 * tps,)), DMA((tps,))],
            compiler_params=pltpu.CompilerParams(collective_id=0, has_side_effects=True, vmem_limit_bytes=GRANT),
        )(*stay(ids, hid, cot, ln_gamma, ln_beta, table, w_in[0], b_in, w_out[0]))
        groups = (vocab // TILE - 1) // 16 + 1
        emb_grad, w1g, b1g, w2g, part = pl.pallas_call(
            functools.partial(grad_kernel, cfg), name='grads',
            out_shape=(S((vocab, dim), F),) + weights + (vec,),
            in_specs=[vmem] * 12, out_specs=[hbm] + [vmem] * 4,
            scratch_shapes=[V((vocab, dim), F), V((dim, toks), F), DMA((groups,))],
            compiler_params=pltpu.CompilerParams(vmem_limit_bytes=GRANT),
        )(*mids)
        sums = pl.pallas_call(
            functools.partial(sum_kernel, cfg), name='sums', out_shape=vec, in_specs=[vmem], out_specs=vmem,
            scratch_shapes=[V(((stages - 2) * tps, 8, LANES), F), DMA((2 * tps,)), DMA(((stages - 2) * tps,))],
            compiler_params=pltpu.CompilerParams(collective_id=1, has_side_effects=True, vmem_limit_bytes=4 << 20),
        )(part)
        gam, bet, loss = pl.pallas_call(
            functools.partial(hand_kernel, cfg), name='hand',
            out_shape=(S((1, dim), F), S((1, dim), F), S((1, 1), F)), in_specs=[vmem], out_specs=[vmem] * 3,
            scratch_shapes=[V((8, LANES), F), DMA, DMA],
            compiler_params=pltpu.CompilerParams(collective_id=2, has_side_effects=True, vmem_limit_bytes=4 << 20),
        )(sums)
        return emb_grad[None], loss.reshape(1), gam, bet, w1g[None], b1g, w2g[None]

    specs_in = (P(lead, None, None), P(lead, None, None, None), P(lead, None, None, None), P(lead, None), P(lead, None), P(lead, 'tp', None), P(lead, None, 'tp'), P(lead, 'tp'), P(lead, 'tp', None))
    specs_out = (P(lead, 'tp', None), P(lead), P(lead, None), P(lead, None), P(lead, None, 'tp'), P(lead, 'tp'), P(lead, 'tp', None))
    return jax.shard_map(body, mesh=mesh, in_specs=specs_in, out_specs=specs_out, check_vma=False)
```

time: 204 us -> 31.7 us (0.16)
  waiting for transfers between devices: 86.9 us -> 0 us
  other arithmetic: 36.6 us -> 0 us
  Pallas kernels: 0 us -> 28.1 us
  local copies, waits for them, and re-layouts: 27.3 us -> 1.02 us
  blocking collectives: 19 us -> 0 us
  matrix products: 14.7 us -> 0 us
  between operations: 15.3 us -> 2.43 us
    psum x2 -> x0, waiting for transfers between devices: 50 us -> none  [the longest x1 33.5 us: body(): d_sum = lax.psum(d_part, 'tp')]
    ppermute x1 -> x0, waiting for transfers between devices: 36.8 us -> none  [body(): recv_grad = lax.ppermute(tab_grad, 'pp', end_pairs)]
    pallas_call x0 -> x4, Pallas kernels: none -> 28.1 us  [the longest x1 13.6 us: body(): pl.pallas_call(functools.partial(stats_kernel, cfg), name='stats', out_sh...]
    another operation x5 -> x0, local copies, waits for them, and re-layouts: 26.3 us -> none
    all_gather x1 -> x0, blocking collectives: 19 us -> none  [body(): stats_all = lax.all_gather(row_stats, 'tp')]
    dot_general x3 -> x0, matrix products: 14.7 us -> none  [the longest x1 5.69 us: last_head(): lax.dot_general(norm_last, vocab_tab, CONTRACT_LAST, preferred_element_ty...]
    convert_element_type x2 -> x0, other arithmetic: 14.1 us -> none  [the longest x1 12.2 us: last_backward(): (exp_local * prob_scale - label_hit.astype(jnp.float32)).astype(jnp.bfloa...]
    reduce_sum x7 -> x0, other arithmetic: 13.4 us -> none  [the longest x1 9.46 us: last_head(): jnp.sum(exp_vals, axis=-1, keepdims=True)]
  transfers between devices with their start and end apart: 3 -> 0, of which waited for: 3 -> 0; matrix products, arithmetic and copies ran while one was open for 1% -> 0% of each run, Pallas kernels for 0% -> 0%
where the time goes in v2:
time: 31.7 us; the launch traced here: 31.6 us
  Pallas kernels  28.1 us (89%)
  between operations  2.43 us (8%)
  local copies, waits for them, and re-layouts  1.02 us (3%)
    pallas_call x1, Pallas kernels, body(): pl.pallas_call(functools.partial(stats_kernel, cfg), name='stats', out_sh...  13.6 us
    pallas_call x1, Pallas kernels, body(): pl.pallas_call(functools.partial(grad_kernel, cfg), name='grads', out_sha...  10.5 us
    pallas_call x1, Pallas kernels, body(): pl.pallas_call(functools.partial(hand_kernel, cfg), name='hand', out_shap...  3.85 us
    unnamed x2, local copies, waits for them, and re-layouts  1.02 us

profile of v2, /device:TPU:7, one launch (start us, length us, event | category | flops | bytes accessed | tf_op | source)
XLA Modules:
  0.0 31.6 jit_solution(9789663837183740839)
XLA Ops:
  0.6 13.6 %stats.1 = (bf16[12576,128]{1,0:T(8,128)(2,1)S(1)}, f32[12576,512]{1,0:T(8,128)S(1)}, bf16[512,128]{1,0:T(8,128)(2,1)S(1)}, s32[8,128]{1,0:T(8,128)S(1)}, f32[8,...) custom-call(s32[4,128]{1,0:T(4,128)} %bitcast.15, ...), custom_call_target="tpu_custom_call" | custom-call | tf_op jit(solution)/shard_map/stats/pallas_call | solution.py:536
  14.2 10.5 %grads.1 = (f32[12576,128]{1,0:T(8,128)}, f32[128,128]{1,0:T(8,128)}, f32[1,128]{1,0:T(1,128)}, f32[128,128]{1,0:T(8,128)}, f32[8,128]{1,0:T(8,128)S(1)}) custom-call(bf16[12576,128]{1,0:T(8,128)(2,1)S(1)} %get-tuple-element.27.e_ref, f32[12576,512]{1,0:T(8,128)S(1)} %get-tuple-element.28.log_ref, bf16[512,128]{1,0:T(8,128)(2,1)S(1)} %get-tuple-element.29.y_ref, ...), custom_call_target="tpu_custom_call" | custom-call | tf_op jit(solution)/shard_map/grads/pallas_call | solution.py:548
  24.7 0.2 sums.1.sum_ref
  24.9 3.9 %hand.1 = (f32[1,128]{1,0:T(1,128)S(1)}, f32[1,128]{1,0:T(1,128)S(1)}, f32[1,1]{1,0:T(1,128)}) custom-call(f32[8,128]{1,0:T(8,128)S(1)} %sums.1.sum_ref), custom_call_target="tpu_custom_call" | custom-call | tf_op jit(solution)/shard_map/hand/pallas_call | solution.py:560
  29.4 0.5 %copy.20 = f32[1,128]{1,0:T(1,128)} copy(f32[1,128]{1,0:T(1,128)S(1)} %get-tuple-element.56) | data formatting | bytes 1024
  29.9 0.5 %copy.21 = f32[1,128]{1,0:T(1,128)} copy(f32[1,128]{1,0:T(1,128)S(1)} %get-tuple-element.57) | data formatting | bytes 1024

commit v3 on v2

--- a/solution.py
+++ b/solution.py
@@ -13,10 +13,13 @@
 LOG2E = 1.4426950408889634
 LANES = 128
 TILE = 256
-SPLIT_STATS = 34
+SPLIT_STATS = 35
 SPLIT_DY = 26
-EARLY = 8
-GRANT = 20 << 20
+EARLY = 4
+FIRST = 32
+PARTS = 4
+DY_LATE = 14
+GRANT = 14 << 20
 MESH = pl.DeviceIdType.MESH
 NT = (((1,), (1,)), ((), ()))
 TN = (((0,), (0,)), ((), ()))
@@ -28,6 +31,19 @@
     return centre * inv, inv
 
 
+def tile_ids(row, size):
+    return (lax.broadcasted_iota(jnp.int32, (size, LANES), 0) + row).astype(jnp.int16)
+
+
+def local_ids(ref, chunks, base, vocab):
+    ids = lanes_row(ref, 0, chunks) - base
+    return jnp.where((ids >= 0) & (ids < vocab), ids, -1).astype(jnp.int16)
+
+
+def steps(count):
+    return max(d for d in range(1, 14) if count % d == 0)
+
+
 def mm(a, b):
     return jnp.dot(a, b, preferred_element_type=F)
 
@@ -37,9 +53,9 @@
 
 
 def stats_kernel(cfg, ids_hbm, hid_hbm, cot_hbm, gam_hbm, bet_hbm, emb_hbm, w1_hbm, b1_hbm, w2_hbm,
-                 e_ref, log_ref, y_out, lab_out, lse_out, dx_out, did_out, xh_out, part_out, w1_out, b1_out, w2_out,
+                 e_ref, log_ref, first_ref, y_out, lab_out, lse_out, dx_out, did_out, xh_out, part_out, w1_out, b1_out, w2_out,
                  ids_ref, hid_ref, cot_ref, gam_ref, bet_ref, w1_ref, b1_ref, w2_ref, ids_smem,
-                 yt_ref, pack_src, pack_dst, dx_src, dx_dst, st_src, st_all, e32_ref, x_ref, part_src, part_all,
+                 yt_ref, buf, pack_src, pack_dst, dx_src, dx_dst, st_src, st_all, e32_ref, x_ref, part_src, part_all,
                  e_sem, in_sem, send_sem, pack_sem, dx_sem, st_sem, part_sem):
     stages, tps, toks, dim, vocab = cfg
     chunks = toks // LANES
@@ -48,7 +64,16 @@
     last = stages - 1
     helper = stages - 2
     full, tail = vocab // TILE - 1, vocab - (vocab // TILE - 1) * TILE
-    e_copy = pltpu.make_async_copy(emb_hbm, e_ref, e_sem)
+    vecs = 2 * chunks
+    half = toks // 2
+    cuts = [i * (full // PARTS) for i in range(PARTS)] + [full]
+
+    def e_part(i):
+        start = cuts[i] * TILE
+        size = (vocab if i == PARTS - 1 else cuts[i + 1] * TILE) - start
+        return pltpu.make_async_copy(emb_hbm.at[pl.ds(start, size)], e_ref.at[pl.ds(start, size)], e_sem.at[i])
+
+    e_parts = [e_part(i) for i in range(PARTS)]
     pairs = ((hid_hbm, hid_ref), (ids_hbm, ids_ref), (gam_hbm, gam_ref), (bet_hbm, bet_ref), (cot_hbm, cot_ref), (ids_hbm, ids_smem), (w1_hbm, w1_ref), (b1_hbm, b1_ref), (w2_hbm, w2_ref))
     hid_ld, ids_ld, gam_ld, bet_ld, cot_ld, smem_ld, w1_ld, b1_ld, w2_ld = [pltpu.make_async_copy(a, b, in_sem.at[i]) for i, (a, b) in enumerate(pairs)]
 
@@ -63,8 +88,17 @@
     def remote(src, dst, ssem, rsem, to_stage, off=0):
         return pltpu.make_async_remote_copy(src, dst, ssem, rsem, device_id={'pp': to_stage, 'tp': lax.rem(rank + off, tps)}, device_id_type=MESH)
 
-    def pack_copy(to_stage, idx, src=None):
-        return remote(pack_src if src is None else src, pack_dst, send_sem.at[idx], pack_sem, to_stage)
+    def pack_rows(which):
+        return pl.ds(0, vecs + half) if which == 0 else pl.ds(vecs + half, half)
+
+    def pack_copy(to_stage, which, idx, src):
+        return remote(src.at[pack_rows(which)], pack_dst.at[pack_rows(which)], send_sem.at[idx], pack_sem.at[which], to_stage)
+
+    def pack_sends():
+        return [pack_copy(helper, 0, 0, pack_src), pack_copy(helper, 1, 1, pack_src), pack_copy(0, 0, 2, pack_src), pack_copy(0, 1, 3, pack_src)]
+
+    def relays():
+        return [pack_copy(1, w, 2 + tps + w, pack_dst) for w in range(2)]
 
     def dx_copy():
         return remote(dx_src, dx_dst, send_sem.at[0], dx_sem, last)
@@ -82,20 +116,27 @@
     def met():
         pl.semaphore_wait(pltpu.get_barrier_semaphore(), stages * tps - 1)
 
-    def normed(rows, gam, bet):
+    def normed(rows, gam, bet, start, size):
         hat, _ = ln_hat(rows)
         norm = (hat * gam + bet).astype(B)
-        xh_out[...] = hat
-        y_out[...] = norm
-        yt_ref[...] = norm.astype(F).T.astype(B)
-
-    def unpack():
-        normed(pack_dst[0:toks, :], pack_dst[toks + chunks:toks + chunks + 1, :], pack_dst[toks + chunks + 1:toks + chunks + 2, :])
-        lab_out[0:chunks, :] = pack_dst[toks:toks + chunks, :].astype(jnp.int32)
+        xh_out[start:start + size, :] = hat
+        y_out[start:start + size, :] = norm
+        yt_ref[:, start:start + size] = norm.astype(F).T.astype(B)
+
+    def unpack(which):
+        start = which * half
+        normed(pack_dst[vecs + start:vecs + start + half, :], pack_dst[chunks:chunks + 1, :], pack_dst[chunks + 1:chunks + 2, :], start, half)
+        if which == 0:
+            lab_out[0:chunks, :] = pack_dst[0:chunks, :].astype(jnp.int32)
+
+    def unpack_all():
+        for w in range(2):
+            pack_copy(helper, w, 0, pack_src).wait_recv()
+            unpack(w)
 
     def st_sends(which):
         slot = 2 * rank + which
-        return [remote(st_src, st_all.at[slot], send_sem.at[2 + i], st_sem.at[slot], lax.rem(stage + ds, stages), off) for i, (ds, off) in enumerate((ds, off) for ds in range(stages) for off in range(tps) if ds or off)]
+        return [remote(st_src, st_all.at[slot], send_sem.at[4 + i], st_sem.at[slot], lax.rem(stage + ds, stages), off) for i, (ds, off) in enumerate((ds, off) for ds in range(stages) for off in range(tps) if ds or off)]
 
     def st_wait(slot):
         remote(st_src, st_all.at[slot], send_sem.at[0], st_sem.at[slot], last).wait_recv()
@@ -116,27 +157,48 @@
         def step(i, carry):
             logit_tile(pl.multiple_of(i * TILE, TILE), TILE)
             return carry
-        lax.fori_loop(first, end, step, 0, unroll=min(8, end - first))
-
-    def logits_to(row, top, size=TILE):
-        return jnp.maximum(top, jnp.max(logit_tile(row, size).reshape(size // 8, 8, toks), axis=0))
-
-    def add_exp(row, top_old, top, tot, size=TILE):
-        ex = jnp.exp(log_ref[pl.ds(row, size), :].reshape(size // 8, 8, toks) - top[None])
+        lax.fori_loop(first, end, step, 0, unroll=steps(end - first))
+
+    def first_tiles(first, end):
+        did = local_ids(did_out, chunks, rank * vocab, vocab)
+
+        def fill(row, size):
+            rows = tile_ids(row, size)
+            one, zero = jnp.ones((size, LANES), B), jnp.zeros((size, LANES), B)
+            h = [jnp.where(rows == did[:, c * LANES:(c + 1) * LANES], one, zero) for c in range(chunks)]
+            first_ref[pl.ds(row, size), :] = mm(jnp.concatenate(h, axis=1), dx_out[...])
+
+        def step(i, carry):
+            fill(pl.multiple_of(i * TILE, TILE), TILE)
+            return carry
+        lax.fori_loop(first, end, step, 0, unroll=steps(end - first))
+        if end == full:
+            fill(full * TILE, tail)
+
+    def logits_to(row, slot, top, size=TILE):
+        logits = logit_tile(row, size)
+        buf[slot, 0:size] = logits
+        return jnp.maximum(top, jnp.max(logits.reshape(size // 8, 8, toks), axis=0))
+
+    def add_exp(slot, top_old, top, tot, size=TILE):
+        ex = jnp.exp(buf[slot, 0:size].reshape(size // 8, 8, toks) - top[None])
         return tot * jnp.exp(top_old - top) + jnp.sum(ex, axis=0)
 
     def begin_stats(first):
         low = jnp.full((8, toks), -jnp.inf, F)
-        top = logits_to(first * TILE, low)
+        top = logits_to(first * TILE, 0, low)
         return top, top, jnp.zeros((8, toks), F)
 
-    def run_stats(first, end, carry):
+    def run_stats(first, pairs, carry):
         def step(i, carry):
             old, top, tot = carry
-            row = pl.multiple_of(i * TILE, TILE)
-            new = logits_to(row + TILE, top)
-            return top, new, add_exp(row, old, top, tot)
-        return lax.fori_loop(first, end, step, carry, unroll=min(8, end - first))
+            row = pl.multiple_of(first * TILE + i * 2 * TILE, TILE)
+            mid = logits_to(row + TILE, 1, top)
+            tot = add_exp(0, old, top, tot)
+            new = logits_to(row + 2 * TILE, 0, mid)
+            tot = add_exp(1, top, mid, tot)
+            return mid, new, tot
+        return lax.fori_loop(0, pairs, step, carry, unroll=min(steps(pairs), 6))
 
     def share_stats(top, tot, which):
         high = jnp.max(top, axis=0, keepdims=True)
@@ -172,52 +234,55 @@
 
     @pl.when(stage == last)
     def _():
-        fetch(hid_ld, ids_ld, gam_ld, bet_ld, e_copy)
+        fetch(hid_ld, ids_ld, gam_ld, bet_ld, *e_parts)
         greet()
         ready(hid_ld, ids_ld, gam_ld, bet_ld)
         rows = hid_ref[...].astype(F)
-        pack_src[0:toks, :] = rows
-        pack_src[toks:toks + chunks, :] = ids_ref[...].astype(F)
-        pack_src[toks + chunks:toks + chunks + 1, :] = gam_ref[...]
-        pack_src[toks + chunks + 1:toks + chunks + 2, :] = bet_ref[...]
-        normed(rows, gam_ref[...], bet_ref[...])
+        pack_src[vecs:vecs + toks, :] = rows
+        pack_src[0:chunks, :] = ids_ref[...].astype(F)
+        pack_src[chunks:chunks + 1, :] = gam_ref[...]
+        pack_src[chunks + 1:chunks + 2, :] = bet_ref[...]
+        pack_src[chunks + 2:vecs, :] = jnp.zeros((vecs - chunks - 2, dim), F)
+        normed(rows, gam_ref[...], bet_ref[...], 0, toks)
         lab_out[0:chunks, :] = ids_ref[...]
-        e_copy.wait()
-        carry = run_stats(0, EARLY, begin_stats(0))
+        e_parts[0].wait()
+        carry = run_stats(0, EARLY // 2, begin_stats(0))
         met()
-        pack_copy(helper, 1).start()
-        pack_copy(0, 0).start()
-        old, top, tot = run_stats(EARLY, SPLIT_STATS - 1, carry)
-        tot = add_exp((SPLIT_STATS - 1) * TILE, old, top, tot)
+        packs = pack_sends()
+        for send in packs:
+            send.start()
+        ready(*e_parts[1:])
+        old, top, tot = run_stats(EARLY, (SPLIT_STATS - 1 - EARLY) // 2, carry)
+        tot = add_exp(0, old, top, tot)
         sends = share_stats(top, tot, 0)
         fill_logits(SPLIT_STATS, full)
         logit_tile(full * TILE, tail)
         dx_copy().wait_recv()
         dx_out[...] = dx_dst[0:toks, :].astype(B)
         did_out[0:chunks, :] = dx_dst[toks:toks + chunks, :].astype(jnp.int32)
+        first_tiles(0, FIRST)
         st_wait(2 * rank + 1)
         for off in range(1, tps):
             st_wait(2 * lax.rem(rank + off, tps))
             st_wait(2 * lax.rem(rank + off, tps) + 1)
         finish_stats()
-        pack_copy(helper, 1).wait_send()
-        pack_copy(0, 0).wait_send()
+        for send in packs:
+            send.wait_send()
         for send in sends:
             send.wait_send()
 
     @pl.when(stage == helper)
     def _():
-        fetch(hid_ld, cot_ld, gam_ld, bet_ld, w1_ld, b1_ld, w2_ld, e_copy)
+        fetch(hid_ld, cot_ld, gam_ld, bet_ld, w1_ld, b1_ld, w2_ld, *e_parts)
         greet()
         mlp()
         met()
-        e_copy.wait()
-        pack_copy(helper, 1).wait_recv()
-        unpack()
-        old, top, tot = run_stats(SPLIT_STATS, full - 1, begin_stats(SPLIT_STATS))
-        new = logits_to(full * TILE, top, tail)
-        tot = add_exp((full - 1) * TILE, old, top, tot)
-        tot = add_exp(full * TILE, top, new, tot, tail)
+        ready(*e_parts)
+        unpack_all()
+        old, top, tot = run_stats(SPLIT_STATS, (full - 1 - SPLIT_STATS) // 2, begin_stats(SPLIT_STATS))
+        new = logits_to(full * TILE, 1, top, tail)
+        tot = add_exp(0, old, top, tot)
+        tot = add_exp(1, top, new, tot, tail)
         sends = share_stats(new, tot, 1)
         fill_logits(SPLIT_DY, SPLIT_STATS)
         st_wait(2 * rank)
@@ -230,17 +295,18 @@
 
     @pl.when(stage == 0)
     def _():
-        fetch(cot_ld, ids_ld, gam_ld, smem_ld, e_copy)
+        fetch(cot_ld, ids_ld, gam_ld, smem_ld, *e_parts)
         greet()
         ready(cot_ld, ids_ld, gam_ld, smem_ld)
-        e_copy.wait()
 
         def widen(i, carry):
             row = pl.multiple_of(i * TILE, TILE)
             e32_ref[pl.ds(row, TILE), :] = e_ref[pl.ds(row, TILE), :].astype(F)
             return carry
 
-        lax.fori_loop(0, full, widen, 0, unroll=4)
+        for i in range(PARTS):
+            e_parts[i].wait()
+            lax.fori_loop(cuts[i], cuts[i + 1], widen, 0, unroll=4)
         e32_ref[full * TILE:vocab, :] = e_ref[full * TILE:vocab, :].astype(F)
         base = rank * vocab
         for c in range(chunks):
@@ -265,13 +331,17 @@
         part_src[1:2, :] = jnp.sum(jnp.where(mask > 0.5, cot, 0.0), axis=0, keepdims=True)
         part_src[2:8, :] = jnp.zeros((6, LANES), F)
         part_all[rank] = part_src[...]
+        first_tiles(0, FIRST // 2)
         met()
         dx_copy().start()
         for off in range(1, tps):
             part_copy(off).start()
-        pack_copy(0, 0).wait_recv()
-        pack_copy(1, 2 + tps, pack_dst).start()
-        unpack()
+        first_tiles(FIRST // 2, full)
+        sends = relays()
+        for w in range(2):
+            pack_copy(0, w, 0, pack_src).wait_recv()
+            sends[w].start()
+            unpack(w)
         fill_logits(0, full)
         logit_tile(full * TILE, tail)
         for off in range(1, tps):
@@ -282,26 +352,63 @@
             st_wait(slot)
         finish_stats()
         dx_copy().wait_send()
-        pack_copy(1, 2 + tps, pack_dst).wait_send()
+        for send in sends:
+            send.wait_send()
         for off in range(1, tps):
             part_copy(off).wait_send()
 
     @pl.when((stage != 0) & (stage != helper) & (stage != last))
     def _():
-        fetch(hid_ld, cot_ld, gam_ld, bet_ld, w1_ld, b1_ld, w2_ld, e_copy)
+        fetch(hid_ld, cot_ld, gam_ld, bet_ld, w1_ld, b1_ld, w2_ld, *e_parts)
         greet()
         mlp()
         met()
-        e_copy.wait()
-        pack_copy(0, 0).wait_recv()
-        unpack()
+        ready(*e_parts)
+        unpack_all()
         fill_logits(0, SPLIT_DY)
         for slot in range(2 * tps):
             st_wait(slot)
         finish_stats()
 
 
-def grad_kernel(cfg, e_ref, log_ref, y_ref, lab_ref, lse_ref, dx_ref, did_ref, xh_ref, pin_ref, w1_in, b1_in, w2_in,
+def dy_piece(cfg, e_ref, log_ref, lab_ref, lse_ref, xh_ref, dyt_ref, part_ref, first, end, with_tail):
+    stages, tps, toks, dim, vocab = cfg
+    chunks = toks // LANES
+    full, tail = vocab // TILE - 1, vocab - (vocab // TILE - 1) * TILE
+    lse = lanes_row(lse_ref, 0, chunks)
+    lab = lanes_row(lab_ref, 0, chunks) - lax.axis_index('tp') * vocab
+    dyt_ref[...] = jnp.zeros((dim, toks), F)
+
+    def work(row, size, seen):
+        x = log_ref[pl.ds(row, size), :] - lse
+        p = jnp.exp2(x * LOG2E)
+        rows = lax.broadcasted_iota(jnp.int32, (size, LANES), 0) + row
+        g, found = [], []
+        for c in range(chunks):
+            cols = slice(c * LANES, (c + 1) * LANES)
+            hit = rows == lab[:, cols]
+            pc, xc, at = p[:, cols], x[:, cols], seen[c]
+            g.append(jnp.where(hit, pc - 1.0, pc).astype(B))
+            for k in range(0, size, 8):
+                at = jnp.where(hit[k:k + 8, :], xc[k:k + 8, :], at)
+            found.append(at)
+        dyt_ref[...] += lax.dot_general(e_ref[pl.ds(row, size), :], jnp.concatenate(g, axis=1), TN, preferred_element_type=F)
+        return tuple(found)
+
+    def step(i, seen):
+        return work(pl.multiple_of(i * TILE, TILE), TILE, seen)
+
+    seen = lax.fori_loop(first, end, step, tuple(jnp.zeros((8, LANES), F) for _ in range(chunks)), unroll=steps(end - first))
+    if with_tail:
+        seen = work(full * TILE, tail, seen)
+    loss = functools.reduce(jnp.add, seen)
+    dy = dyt_ref[...].T
+    part_ref[2:3, :] += jnp.sum(dy * xh_ref[...], axis=0, keepdims=True)
+    part_ref[3:4, :] += jnp.sum(dy, axis=0, keepdims=True)
+    part_ref[4:5, :] += jnp.sum(loss, axis=0, keepdims=True)
+
+
+def grad_kernel(cfg, e_ref, log_ref, first_ref, y_ref, lab_ref, lse_ref, dx_ref, did_ref, xh_ref, pin_ref, w1_in, b1_in, w2_in,
                 emb_out, w1_out, b1_out, w2_out, part_out, out_ref, dyt_ref, o_sem):
     stages, tps, toks, dim, vocab = cfg
     chunks = toks // LANES
@@ -322,34 +429,49 @@
         w2_out[...] = jnp.zeros(w2_out.shape, F)
         part_out[...] = pin_ref[...]
         lse = lanes_row(lse_ref, 0, chunks)
-        lab = (lanes_row(lab_ref, 0, chunks) - base)
-        did = (lanes_row(did_ref, 0, chunks) - base)
-        lab = jnp.where((lab >= 0) & (lab < vocab), lab, -1).astype(jnp.int16)
-        did = jnp.where((did >= 0) & (did < vocab), did, -1).astype(jnp.int16)
+        lab = local_ids(lab_ref, chunks, base, vocab)
+        did = local_ids(did_ref, chunks, base, vocab)
 
         def out_copy(c):
             size = tail if c == groups else size16
             return pltpu.make_async_copy(out_ref.at[pl.ds(c * size16, size)], emb_out.at[pl.ds(c * size16, size)], o_sem.at[c])
 
-        def work(row, size):
+        def work(row, size, pick):
             p = jnp.exp2((log_ref[pl.ds(row, size), :] - lse) * LOG2E)
-            rows = (lax.broadcasted_iota(jnp.int32, (size, LANES), 0) + row).astype(jnp.int16)
+            rows = tile_ids(row, size)
             one, zero = jnp.ones((size, LANES), B), jnp.zeros((size, LANES), B)
             g, h = [], []
             for c in range(chunks):
                 cols = slice(c * LANES, (c + 1) * LANES)
                 pc = p[:, cols]
                 g.append(jnp.where(rows == lab[:, cols], (pc - 1.0).astype(B), pc.astype(B)))
-                h.append(jnp.where(rows == did[:, cols], one, zero))
-            out_ref[pl.ds(row, size), :] = mm(jnp.concatenate(g, axis=1), y_ref[...]) + mm(jnp.concatenate(h, axis=1), dx_ref[...])
+                if pick:
+                    h.append(jnp.where(rows == did[:, cols], one, zero))
+            first = mm(jnp.concatenate(h, axis=1), dx_ref[...]) if pick else first_ref[pl.ds(row, size), :]
+            out_ref[pl.ds(row, size), :] = first + mm(jnp.concatenate(g, axis=1), y_ref[...])
+
+        def sweep(first, end, pick):
+            def step(i, carry):
+                work(pl.multiple_of(i * TILE, TILE), TILE, pick)
+                return carry
+            lax.fori_loop(first, end, step, 0, unroll=steps(end - first) if pick else 16)
 
         for c in range(groups):
-            def step(i, carry):
-                work(pl.multiple_of(c * size16 + i * TILE, TILE), TILE)
-                return carry
-            lax.fori_loop(0, group, step, 0, unroll=16)
+            if (c + 1) * group <= FIRST:
+                sweep(c * group, (c + 1) * group, False)
+            else:
+                @pl.when(stage == 0)
+                def _():
+                    sweep(c * group, (c + 1) * group, False)
+                    if c == groups - 1:
+                        work(full * TILE, tail, False)
+
+                @pl.when(stage != 0)
+                def _():
+                    sweep(c * group, (c + 1) * group, True)
+                    if c == groups - 1:
+                        work(full * TILE, tail, True)
             out_copy(c).start()
-        work(full * TILE, tail)
         out_copy(groups).start()
         for c in range(groups + 1):
             out_copy(c).wait()
@@ -368,49 +490,21 @@
         b1_out[...] = b1_in[...]
         w2_out[...] = w2_in[...]
         part_out[...] = pin_ref[...]
-        lse = lanes_row(lse_ref, 0, chunks)
-        lab = lanes_row(lab_ref, 0, chunks) - base
-        dyt_ref[...] = jnp.zeros((dim, toks), F)
-
-        def work(row, size, loss):
-            x = log_ref[pl.ds(row, size), :] - lse
-            p = jnp.exp2(x * LOG2E)
-            rows = lax.broadcasted_iota(jnp.int32, (size, LANES), 0) + row
-            g, picked = [], []
-            for c in range(chunks):
-                cols = slice(c * LANES, (c + 1) * LANES)
-                hit = rows == lab[:, cols]
-                pc = p[:, cols]
-                g.append(jnp.where(hit, pc - 1.0, pc).astype(B))
-                picked.append(jnp.sum(jnp.where(hit, x[:, cols], 0.0).reshape(size // 8, 8, LANES), axis=0))
-            dyt_ref[...] += lax.dot_general(e_ref[pl.ds(row, size), :], jnp.concatenate(g, axis=1), TN, preferred_element_type=F)
-            return loss + functools.reduce(jnp.add, picked)
-
-        def sweep(first, end, loss):
-            def step(i, loss):
-                return work(pl.multiple_of(i * TILE, TILE), TILE, loss)
-            return lax.fori_loop(first, end, step, loss, unroll=min(8, end - first))
-
-        def finish(loss):
-            dy = dyt_ref[...].T
-            part_out[2:3, :] = jnp.sum(dy * xh_ref[...], axis=0, keepdims=True)
-            part_out[3:4, :] = jnp.sum(dy, axis=0, keepdims=True)
-            part_out[4:5, :] = jnp.sum(loss, axis=0, keepdims=True)
+        pieces = functools.partial(dy_piece, cfg, e_ref, log_ref, lab_ref, lse_ref, xh_ref, dyt_ref, part_out)
 
         @pl.when(stage == helper)
         def _():
-            loss = sweep(SPLIT_DY, full, jnp.zeros((8, LANES), F))
-            finish(work(full * TILE, tail, loss))
+            pieces(SPLIT_DY + DY_LATE, full, True)
 
         @pl.when(stage != helper)
         def _():
-            finish(sweep(0, SPLIT_DY, jnp.zeros((8, LANES), F)))
+            pieces(DY_LATE, SPLIT_DY, False)
 
         for c in range(groups + 1):
             zero_copy(c).wait()
 
 
-def sum_kernel(cfg, part_ref, sum_out, got, send_sem, recv_sem):
+def sum_kernel(cfg, e_ref, log_ref, lab_ref, lse_ref, xh_ref, pin_ref, sum_out, part_ref, dyt_ref, got, send_sem, recv_sem):
     stages, tps, toks, dim, vocab = cfg
     rank = lax.axis_index('tp')
     stage = lax.axis_index('pp')
@@ -436,6 +530,16 @@
                 @pl.when((stage != to_stage) | (off != 0))
                 def _():
                     pl.semaphore_signal(bar, inc=1, device_id={'pp': to_stage, 'tp': lax.rem(rank + off, tps)}, device_id_type=MESH)
+        part_ref[...] = pin_ref[...]
+        pieces = functools.partial(dy_piece, cfg, e_ref, log_ref, lab_ref, lse_ref, xh_ref, dyt_ref, part_ref)
+
+        @pl.when(stage == helper)
+        def _():
+            pieces(SPLIT_DY, SPLIT_DY + DY_LATE, False)
+
+        @pl.when(stage != helper)
+        def _():
+            pieces(0, DY_LATE, False)
         pl.semaphore_wait(bar, mids * tps - 1)
 
         @pl.when(stage == helper)
@@ -470,10 +574,10 @@
 
     @pl.when((stage == 0) | (stage == last))
     def _():
-        sum_out[...] = part_ref[...]
-
-
-def hand_kernel(cfg, sum_ref, gam_out, bet_out, loss_out, got, send_sem, recv_sem):
+        sum_out[...] = pin_ref[...]
+
+
+def hand_kernel(cfg, sum_ref, vec_out, got, send_sem, recv_sem):
     stages, tps, toks, dim, vocab = cfg
     stage = lax.axis_index('pp')
     last = stages - 1
@@ -492,18 +596,22 @@
 
     @pl.when(stage != last)
     def _():
-        gam_out[...] = sum_ref[0:1, :]
-        bet_out[...] = sum_ref[1:2, :]
-        loss_out[...] = jnp.zeros((1, 1), F)
+        vec_out[0:2, :] = sum_ref[0:2, :]
+        vec_out[2:3, :] = jnp.zeros((1, LANES), F)
 
     @pl.when(stage == last)
     def _():
         pl.semaphore_signal(bar, inc=1, device_id={'pp': helper}, device_id_type=MESH)
         pl.semaphore_wait(bar, 1)
         hand_over().wait_recv()
-        gam_out[...] = got[2:3, :]
-        bet_out[...] = got[3:4, :]
-        loss_out[...] = jnp.sum(got[4:5, :], axis=1, keepdims=True) * (-1.0 / toks)
+        vec_out[0:2, :] = got[2:4, :]
+        vec_out[2:3, :] = got[4:5, :] * (-1.0 / toks)
+
+
+def write_kernel(vec_ref, gam_out, bet_out, loss_out):
+    gam_out[...] = vec_ref[0:1, :]
+    bet_out[...] = vec_ref[1:2, :]
+    loss_out[0] = jnp.sum(vec_ref[2:3, :])
 
 
 def solution(mesh):
@@ -535,35 +643,38 @@
         weights = (S((dim, ff), F), S((1, ff), F), S((ff, dim), F))
         mids = pl.pallas_call(
             functools.partial(stats_kernel, cfg), name='stats',
-            out_shape=(S((vocab, dim), B), S((vocab, toks), F), S((toks, dim), B), S((8, LANES), I), vec, S((toks, dim), B), S((8, LANES), I), S((toks, dim), F), vec) + weights,
-            in_specs=[hbm] * 9, out_specs=[vmem] * 12,
+            out_shape=(S((vocab, dim), B), S((vocab, toks), F), S((vocab, dim), F), S((toks, dim), B), S((8, LANES), I), vec, S((toks, dim), B), S((8, LANES), I), S((toks, dim), F), vec) + weights,
+            in_specs=[hbm] * 9, out_specs=[vmem] * 13,
             scratch_shapes=[
                 V((chunks, LANES), I), V((toks, dim), B), V((toks, dim), B), V((1, dim), F), V((1, dim), F), V((dim, ff), B), V((1, ff), F), V((ff, dim), B), pltpu.SMEM((chunks, LANES), I),
-                V((dim, toks), B), V((rows, dim), F), V((rows, dim), F), V((rows, dim), F), V((rows, dim), F),
+                V((dim, toks), B), V((2, TILE + 32, toks), F), V((rows, dim), F), V((rows, dim), F), V((rows, dim), F), V((rows, dim), F),
                 V((8, LANES), F), V((2 * tps, 8, LANES), F), V((vocab, dim), F), V((toks, dim), F), V((8, LANES), F), V((tps, 8, LANES), F),
-                DMA, DMA((9,)), DMA((2 + stages * tps,)), DMA, DMA, DMA((2 * tps,)), DMA((tps,))],
+                DMA((PARTS,)), DMA((9,)), DMA((4 + stages * tps,)), DMA((2,)), DMA, DMA((2 * tps,)), DMA((tps,))],
             compiler_params=pltpu.CompilerParams(collective_id=0, has_side_effects=True, vmem_limit_bytes=GRANT),
         )(*stay(ids, hid, cot, ln_gamma, ln_beta, table, w_in[0], b_in, w_out[0]))
         groups = (vocab // TILE - 1) // 16 + 1
         emb_grad, w1g, b1g, w2g, part = pl.pallas_call(
             functools.partial(grad_kernel, cfg), name='grads',
             out_shape=(S((vocab, dim), F),) + weights + (vec,),
-            in_specs=[vmem] * 12, out_specs=[hbm] + [vmem] * 4,
+            in_specs=[vmem] * 13, out_specs=[hbm] + [vmem] * 4,
             scratch_shapes=[V((vocab, dim), F), V((dim, toks), F), DMA((groups,))],
             compiler_params=pltpu.CompilerParams(vmem_limit_bytes=GRANT),
         )(*mids)
         sums = pl.pallas_call(
-            functools.partial(sum_kernel, cfg), name='sums', out_shape=vec, in_specs=[vmem], out_specs=vmem,
-            scratch_shapes=[V(((stages - 2) * tps, 8, LANES), F), DMA((2 * tps,)), DMA(((stages - 2) * tps,))],
-            compiler_params=pltpu.CompilerParams(collective_id=1, has_side_effects=True, vmem_limit_bytes=4 << 20),
-        )(part)
-        gam, bet, loss = pl.pallas_call(
-            functools.partial(hand_kernel, cfg), name='hand',
-            out_shape=(S((1, dim), F), S((1, dim), F), S((1, 1), F)), in_specs=[vmem], out_specs=[vmem] * 3,
+            functools.partial(sum_kernel, cfg), name='sums', out_shape=vec, in_specs=[vmem] * 6, out_specs=vmem,
+            scratch_shapes=[V((8, LANES), F), V((dim, toks), F), V(((stages - 2) * tps, 8, LANES), F), DMA((2 * tps,)), DMA(((stages - 2) * tps,))],
+            compiler_params=pltpu.CompilerParams(collective_id=1, has_side_effects=True, vmem_limit_bytes=GRANT),
+        )(mids[0], mids[1], mids[4], mids[5], mids[8], part)
+        vecs = pl.pallas_call(
+            functools.partial(hand_kernel, cfg), name='hand', out_shape=vec, in_specs=[vmem], out_specs=vmem,
             scratch_shapes=[V((8, LANES), F), DMA, DMA],
             compiler_params=pltpu.CompilerParams(collective_id=2, has_side_effects=True, vmem_limit_bytes=4 << 20),
         )(sums)
-        return emb_grad[None], loss.reshape(1), gam, bet, w1g[None], b1g, w2g[None]
+        gam, bet, loss = pl.pallas_call(
+            write_kernel, name='write', out_shape=(S((1, dim), F), S((1, dim), F), S((1,), F)), in_specs=[vmem], out_specs=[vmem] * 2 + [pl.BlockSpec(memory_space=pltpu.SMEM)],
+            compiler_params=pltpu.CompilerParams(vmem_limit_bytes=4 << 20),
+        )(vecs)
+        return emb_grad[None], loss, gam, bet, w1g[None], b1g, w2g[None]
 
     specs_in = (P(lead, None, None), P(lead, None, None, None), P(lead, None, None, None), P(lead, None), P(lead, None), P(lead, 'tp', None), P(lead, None, 'tp'), P(lead, 'tp'), P(lead, 'tp', None))
     specs_out = (P(lead, 'tp', None), P(lead), P(lead, None), P(lead, None), P(lead, None, 'tp'), P(lead, 'tp'), P(lead, 'tp', None))

time: 31.7 us -> 27.5 us (0.87)
  Pallas kernels: 28.1 us -> 26.5 us
  between operations: 2.43 us -> 0.85 us
  local copies, waits for them, and re-layouts: 1.02 us -> 0 us
    pallas_call x1, Pallas kernels: 3.85 us -> 1.23 us  [body(): pl.pallas_call(functools.partial(hand_kernel, cfg), name='hand', out_shap...]
    unnamed x2 -> x0, local copies, waits for them, and re-layouts: 1.02 us -> none
    pallas_call x1, Pallas kernels: 13.6 us -> 14.5 us  [body(): pl.pallas_call(functools.partial(stats_kernel, cfg), name='stats', out_sh...]
    pallas_call x0 -> x1, Pallas kernels: none -> 0.63 us  [body(): pl.pallas_call(write_kernel, name='write', out_shape=(S((1, dim), F), S((...]
    pallas_call x1, Pallas kernels: 10.5 us -> 10 us  [body(): pl.pallas_call(functools.partial(grad_kernel, cfg), name='grads', out_sha...]
where the time goes in v3:
time: 27.5 us; the launch traced here: 27.4 us
  Pallas kernels  26.5 us (96%)
  between operations  0.85 us (3%)
    pallas_call x1, Pallas kernels, body(): pl.pallas_call(functools.partial(stats_kernel, cfg), name='stats', out_sh...  14.5 us
    pallas_call x1, Pallas kernels, body(): pl.pallas_call(functools.partial(grad_kernel, cfg), name='grads', out_sha...  10 us
    pallas_call x1, Pallas kernels, body(): pl.pallas_call(functools.partial(hand_kernel, cfg), name='hand', out_shap...  1.23 us
    pallas_call x1, Pallas kernels, body(): pl.pallas_call(write_kernel, name='write', out_shape=(S((1, dim), F), S((...  0.63 us

profile of v3, /device:TPU:7, one launch (start us, length us, event | category | flops | bytes accessed | tf_op | source)
XLA Modules:
  0.0 27.4 jit_solution(17039709830570324060)
XLA Ops:
  0.6 14.5 %stats.1 = (bf16[12576,128]{1,0:T(8,128)(2,1)S(1)}, f32[12576,512]{1,0:T(8,128)S(1)}, f32[12576,128]{1,0:T(8,128)S(1)}, bf16[512,128]{1,0:T(8,128)(2,1)S(1)}, s3...) custom-call(s32[4,128]{1,0:T(4,128)} %bitcast.14, ...), custom_call_target="tpu_custom_call" | custom-call | tf_op jit(solution)/shard_map/stats/pallas_call | solution.py:644
  15.1 10.0 %grads.1 = (f32[12576,128]{1,0:T(8,128)}, f32[128,128]{1,0:T(8,128)}, f32[1,128]{1,0:T(1,128)}, f32[128,128]{1,0:T(8,128)}, f32[8,128]{1,0:T(8,128)S(1)}) custom-call(bf16[12576,128]{1,0:T(8,128)(2,1)S(1)} %get-tuple-element.28.e_ref, f32[12576,512]{1,0:T(8,128)S(1)} %get-tuple-element.29.log_ref, f32[12576,128]{1,0:T(8,128)S(1)} %get-tuple-element.30.first_ref, ...), custom_call_target="tpu_custom_call" | custom-call | tf_op jit(solution)/shard_map/grads/pallas_call | solution.py:656
  25.1 0.2 sums.1.sum_ref
  25.3 1.2 %hand.1.vec_ref = f32[8,128]{1,0:T(8,128)S(1)} custom-call(f32[8,128]{1,0:T(8,128)S(1)} %sums.1.sum_ref), custom_call_target="tpu_custom_call" | custom-call | tf_op jit(solution)/shard_map/hand/pallas_call | solution.py:668
  26.6 0.6 %write.1 = (f32[1,128]{1,0:T(1,128)}, f32[1,128]{1,0:T(1,128)}, f32[1]{0:T(128)}) custom-call(f32[8,128]{1,0:T(8,128)S(1)} %hand.1.vec_ref), custom_call_target="tpu_custom_call" | custom-call | tf_op jit(solution)/shard_map/write/pallas_call | solution.py:673

commit v4 on v3

--- a/solution.py
+++ b/solution.py
@@ -13,12 +13,14 @@
 LOG2E = 1.4426950408889634
 LANES = 128
 TILE = 256
-SPLIT_STATS = 35
-SPLIT_DY = 26
-EARLY = 4
-FIRST = 32
+SPLIT_STATS = 37
+SPLIT_DY = 16
+EARLY = 8
+FIRST = 16
+FRESH = 48
 PARTS = 4
-DY_LATE = 14
+LATE_HELPER = 16
+LATE_FIRST = 6
 GRANT = 14 << 20
 MESH = pl.DeviceIdType.MESH
 NT = (((1,), (1,)), ((), ()))
@@ -53,10 +55,10 @@
 
 
 def stats_kernel(cfg, ids_hbm, hid_hbm, cot_hbm, gam_hbm, bet_hbm, emb_hbm, w1_hbm, b1_hbm, w2_hbm,
-                 e_ref, log_ref, first_ref, y_out, lab_out, lse_out, dx_out, did_out, xh_out, part_out, w1_out, b1_out, w2_out,
+                 e_ref, log_ref, first_ref, y_out, lab_out, lse_out, dx_out, did_out, xh_out, part_out, w1_out, w2_out, yt_ref,
                  ids_ref, hid_ref, cot_ref, gam_ref, bet_ref, w1_ref, b1_ref, w2_ref, ids_smem,
-                 yt_ref, buf, pack_src, pack_dst, dx_src, dx_dst, st_src, st_all, e32_ref, x_ref, part_src, part_all,
-                 e_sem, in_sem, send_sem, pack_sem, dx_sem, st_sem, part_sem):
+                 buf, pack_src, pack_dst, dx_src, dx_dst, st_src, st_all, e32_ref, x_ref, part_src, part_all,
+                 e_sem, in_sem, send_sem, many_sem, pack_sem, dx_sem, st_sem, part_sem):
     stages, tps, toks, dim, vocab = cfg
     chunks = toks // LANES
     rank = lax.axis_index('tp')
@@ -98,13 +100,13 @@
         return [pack_copy(helper, 0, 0, pack_src), pack_copy(helper, 1, 1, pack_src), pack_copy(0, 0, 2, pack_src), pack_copy(0, 1, 3, pack_src)]
 
     def relays():
-        return [pack_copy(1, w, 2 + tps + w, pack_dst) for w in range(2)]
+        return [pack_copy(1, w, 1 + w, pack_dst) for w in range(2)]
 
     def dx_copy():
         return remote(dx_src, dx_dst, send_sem.at[0], dx_sem, last)
 
     def part_copy(off):
-        return remote(part_src, part_all.at[rank], send_sem.at[off], part_sem.at[rank], 0, off)
+        return remote(part_src, part_all.at[rank], many_sem, part_sem, 0, off)
 
     def greet():
         bar = pltpu.get_barrier_semaphore()
@@ -136,10 +138,15 @@
 
     def st_sends(which):
         slot = 2 * rank + which
-        return [remote(st_src, st_all.at[slot], send_sem.at[4 + i], st_sem.at[slot], lax.rem(stage + ds, stages), off) for i, (ds, off) in enumerate((ds, off) for ds in range(stages) for off in range(tps) if ds or off)]
-
-    def st_wait(slot):
-        remote(st_src, st_all.at[slot], send_sem.at[0], st_sem.at[slot], last).wait_recv()
+        return [remote(st_src, st_all.at[slot], many_sem, st_sem, lax.rem(stage + ds, stages), off) for ds in range(stages) for off in range(tps) if ds or off]
+
+    def st_wait(count):
+        got = st_all.at[pl.ds(0, count)]
+        remote(got, got, many_sem, st_sem, last).wait_recv()
+
+    def st_sent():
+        sent = pack_src.at[pl.ds(0, 8 * (stages * tps - 1))]
+        remote(sent, sent, many_sem, st_sem, last).wait_send()
 
     def finish_stats():
         tops = [st_all[r, 0:chunks, :] for r in range(2 * tps)]
@@ -198,7 +205,7 @@
             new = logits_to(row + 2 * TILE, 0, mid)
             tot = add_exp(1, top, mid, tot)
             return mid, new, tot
-        return lax.fori_loop(0, pairs, step, carry, unroll=min(steps(pairs), 6))
+        return lax.fori_loop(0, pairs, step, carry, unroll=steps(pairs))
 
     def share_stats(top, tot, which):
         high = jnp.max(top, axis=0, keepdims=True)
@@ -207,10 +214,8 @@
             st_src[c:c + 1, :] = high[:, c * LANES:(c + 1) * LANES]
             st_src[chunks + c:chunks + c + 1, :] = tot[:, c * LANES:(c + 1) * LANES]
         st_all[2 * rank + which] = st_src[...]
-        sends = st_sends(which)
-        for send in sends:
+        for send in st_sends(which):
             send.start()
-        return sends
 
     def mlp():
         ready(hid_ld, cot_ld, gam_ld, bet_ld, w1_ld, b1_ld, w2_ld)
@@ -226,17 +231,19 @@
         d_pre = d_act * slope
         d_b = d_pre.astype(B)
         w1_out[...] = lax.dot_general(norm, d_b, TN, preferred_element_type=F)
-        b1_out[...] = jnp.sum(d_pre, axis=0, keepdims=True)
+        part_out[5:6, :] = jnp.sum(d_pre, axis=0, keepdims=True)
         d_h = lax.dot_general(d_b, w1_ref[...], NT, preferred_element_type=F)
         part_out[0:1, :] = jnp.sum(d_h * hat, axis=0, keepdims=True)
         part_out[1:2, :] = jnp.sum(d_h, axis=0, keepdims=True)
-        part_out[2:8, :] = jnp.zeros((6, LANES), F)
+        part_out[2:5, :] = jnp.zeros((3, LANES), F)
+        part_out[6:8, :] = jnp.zeros((2, LANES), F)
 
     @pl.when(stage == last)
     def _():
-        fetch(hid_ld, ids_ld, gam_ld, bet_ld, *e_parts)
+        fetch(hid_ld, ids_ld, gam_ld, bet_ld, e_parts[0])
         greet()
         ready(hid_ld, ids_ld, gam_ld, bet_ld)
+        fetch(*e_parts[1:])
         rows = hid_ref[...].astype(F)
         pack_src[vecs:vecs + toks, :] = rows
         pack_src[0:chunks, :] = ids_ref[...].astype(F)
@@ -254,22 +261,18 @@
         ready(*e_parts[1:])
         old, top, tot = run_stats(EARLY, (SPLIT_STATS - 1 - EARLY) // 2, carry)
         tot = add_exp(0, old, top, tot)
-        sends = share_stats(top, tot, 0)
+        share_stats(top, tot, 0)
         fill_logits(SPLIT_STATS, full)
         logit_tile(full * TILE, tail)
         dx_copy().wait_recv()
         dx_out[...] = dx_dst[0:toks, :].astype(B)
         did_out[0:chunks, :] = dx_dst[toks:toks + chunks, :].astype(jnp.int32)
         first_tiles(0, FIRST)
-        st_wait(2 * rank + 1)
-        for off in range(1, tps):
-            st_wait(2 * lax.rem(rank + off, tps))
-            st_wait(2 * lax.rem(rank + off, tps) + 1)
+        st_wait(2 * tps - 1)
         finish_stats()
         for send in packs:
             send.wait_send()
-        for send in sends:
-            send.wait_send()
+        st_sent()
 
     @pl.when(stage == helper)
     def _():
@@ -283,15 +286,11 @@
         new = logits_to(full * TILE, 1, top, tail)
         tot = add_exp(0, old, top, tot)
         tot = add_exp(1, top, new, tot, tail)
-        sends = share_stats(new, tot, 1)
+        share_stats(new, tot, 1)
         fill_logits(SPLIT_DY, SPLIT_STATS)
-        st_wait(2 * rank)
-        for off in range(1, tps):
-            st_wait(2 * lax.rem(rank + off, tps))
-            st_wait(2 * lax.rem(rank + off, tps) + 1)
+        st_wait(2 * tps - 1)
         finish_stats()
-        for send in sends:
-            send.wait_send()
+        st_sent()
 
     @pl.when(stage == 0)
     def _():
@@ -331,12 +330,11 @@
         part_src[1:2, :] = jnp.sum(jnp.where(mask > 0.5, cot, 0.0), axis=0, keepdims=True)
         part_src[2:8, :] = jnp.zeros((6, LANES), F)
         part_all[rank] = part_src[...]
-        first_tiles(0, FIRST // 2)
         met()
         dx_copy().start()
         for off in range(1, tps):
             part_copy(off).start()
-        first_tiles(FIRST // 2, full)
+        first_tiles(0, full)
         sends = relays()
         for w in range(2):
             pack_copy(0, w, 0, pack_src).wait_recv()
@@ -344,18 +342,15 @@
             unpack(w)
         fill_logits(0, full)
         logit_tile(full * TILE, tail)
-        for off in range(1, tps):
-            src = lax.rem(rank + off, tps)
-            remote(part_src, part_all.at[src], send_sem.at[0], part_sem.at[src], 0).wait_recv()
+        others = part_all.at[pl.ds(0, tps - 1)]
+        remote(others, others, many_sem, part_sem, 0, 1).wait_recv()
         part_out[...] = functools.reduce(jnp.add, [part_all[r] for r in range(tps)])
-        for slot in range(2 * tps):
-            st_wait(slot)
+        st_wait(2 * tps)
         finish_stats()
         dx_copy().wait_send()
         for send in sends:
             send.wait_send()
-        for off in range(1, tps):
-            part_copy(off).wait_send()
+        remote(others, others, many_sem, part_sem, 0, 1).wait_send()
 
     @pl.when((stage != 0) & (stage != helper) & (stage != last))
     def _():
@@ -366,8 +361,7 @@
         ready(*e_parts)
         unpack_all()
         fill_logits(0, SPLIT_DY)
-        for slot in range(2 * tps):
-            st_wait(slot)
+        st_wait(2 * tps)
         finish_stats()
 
 
@@ -408,8 +402,8 @@
     part_ref[4:5, :] += jnp.sum(loss, axis=0, keepdims=True)
 
 
-def grad_kernel(cfg, e_ref, log_ref, first_ref, y_ref, lab_ref, lse_ref, dx_ref, did_ref, xh_ref, pin_ref, w1_in, b1_in, w2_in,
-                emb_out, w1_out, b1_out, w2_out, part_out, out_ref, dyt_ref, o_sem):
+def grad_kernel(cfg, e_ref, log_ref, first_ref, y_ref, lab_ref, lse_ref, dx_ref, did_ref, xh_ref, pin_ref, w1_in, w2_in, yt_ref,
+                emb_out, w1_out, b1_out, w2_out, part_out, out_ref, dyt_ref, zero_ref, bias_ref, o_sem, w_sem):
     stages, tps, toks, dim, vocab = cfg
     chunks = toks // LANES
     rank = lax.axis_index('tp')
@@ -418,26 +412,32 @@
     helper = stages - 2
     base = rank * vocab
     full, tail = vocab // TILE - 1, vocab - (vocab // TILE - 1) * TILE
-    group = 16
-    groups = full // group
-    size16 = group * TILE
+    bounds = (0, 16, 32, 44, full)
+    spans = [(bounds[i], bounds[i + 1]) for i in range(4)]
+    size16 = 16 * TILE
+
+    def small(w1_src, w2_src):
+        return [pltpu.make_async_copy(w1_src, w1_out, w_sem.at[0]), pltpu.make_async_copy(bias_ref, b1_out, w_sem.at[1]), pltpu.make_async_copy(w2_src, w2_out, w_sem.at[2])]
 
     @pl.when((stage == 0) | (stage == last))
     def _():
-        w1_out[...] = jnp.zeros(w1_out.shape, F)
-        b1_out[...] = jnp.zeros(b1_out.shape, F)
-        w2_out[...] = jnp.zeros(w2_out.shape, F)
+        zero_ref[...] = jnp.zeros(zero_ref.shape, F)
+        bias_ref[...] = jnp.zeros(bias_ref.shape, F)
+        smalls = small(zero_ref, zero_ref)
+        for copy in smalls:
+            copy.start()
         part_out[...] = pin_ref[...]
         lse = lanes_row(lse_ref, 0, chunks)
         lab = local_ids(lab_ref, chunks, base, vocab)
         did = local_ids(did_ref, chunks, base, vocab)
 
         def out_copy(c):
-            size = tail if c == groups else size16
-            return pltpu.make_async_copy(out_ref.at[pl.ds(c * size16, size)], emb_out.at[pl.ds(c * size16, size)], o_sem.at[c])
-
-        def work(row, size, pick):
-            p = jnp.exp2((log_ref[pl.ds(row, size), :] - lse) * LOG2E)
+            start, size = (full * TILE, tail) if c == len(spans) else (spans[c][0] * TILE, (spans[c][1] - spans[c][0]) * TILE)
+            return pltpu.make_async_copy(out_ref.at[pl.ds(start, size)], emb_out.at[pl.ds(start, size)], o_sem.at[c])
+
+        def work(row, size, pick, fresh):
+            logits = mm(e_ref[pl.ds(row, size), :], yt_ref[...]) if fresh else log_ref[pl.ds(row, size), :]
+            p = jnp.exp2((logits - lse) * LOG2E)
             rows = tile_ids(row, size)
             one, zero = jnp.ones((size, LANES), B), jnp.zeros((size, LANES), B)
             g, h = [], []
@@ -450,58 +450,51 @@
             first = mm(jnp.concatenate(h, axis=1), dx_ref[...]) if pick else first_ref[pl.ds(row, size), :]
             out_ref[pl.ds(row, size), :] = first + mm(jnp.concatenate(g, axis=1), y_ref[...])
 
-        def sweep(first, end, pick):
+        def sweep(first, end, pick, fresh=False):
             def step(i, carry):
-                work(pl.multiple_of(i * TILE, TILE), TILE, pick)
+                work(pl.multiple_of(i * TILE, TILE), TILE, pick, fresh)
                 return carry
-            lax.fori_loop(first, end, step, 0, unroll=steps(end - first) if pick else 16)
-
-        for c in range(groups):
-            if (c + 1) * group <= FIRST:
-                sweep(c * group, (c + 1) * group, False)
+            lax.fori_loop(first, end, step, 0, unroll=min(16, end - first))
+
+        def both(run, fresh):
+            pl.when(stage == 0)(lambda: run(False, fresh))
+            pl.when(stage != 0)(lambda: run(True, False))
+
+        both(lambda pick, fresh: work(full * TILE, tail, pick, fresh), False)
+        out_copy(len(spans)).start()
+        for c, (first, end) in enumerate(spans):
+            if end <= FIRST:
+                sweep(first, end, False)
             else:
-                @pl.when(stage == 0)
-                def _():
-                    sweep(c * group, (c + 1) * group, False)
-                    if c == groups - 1:
-                        work(full * TILE, tail, False)
-
-                @pl.when(stage != 0)
-                def _():
-                    sweep(c * group, (c + 1) * group, True)
-                    if c == groups - 1:
-                        work(full * TILE, tail, True)
+                both(functools.partial(sweep, first, end), first >= FRESH)
             out_copy(c).start()
-        out_copy(groups).start()
-        for c in range(groups + 1):
+        for c in range(len(spans) + 1):
             out_copy(c).wait()
+        for copy in smalls:
+            copy.wait()
 
     @pl.when((stage != 0) & (stage != last))
     def _():
         out_ref[0:size16, :] = jnp.zeros((size16, dim), F)
 
-        def zero_copy(c):
-            n = tail if c == groups else size16
-            return pltpu.make_async_copy(out_ref.at[pl.ds(0, n)], emb_out.at[pl.ds(c * size16, n)], o_sem.at[c])
-
-        for c in range(groups + 1):
-            zero_copy(c).start()
-        w1_out[...] = w1_in[...]
-        b1_out[...] = b1_in[...]
-        w2_out[...] = w2_in[...]
+        bias_ref[...] = pin_ref[5:6, :]
+        zeros = [pltpu.make_async_copy(out_ref.at[pl.ds(0, n)], emb_out.at[pl.ds(c * size16, n)], o_sem.at[c]) for c, n in enumerate((size16, size16, size16, tail))]
+        smalls = small(w1_in, w2_in)
+        for copy in zeros + smalls:
+            copy.start()
         part_out[...] = pin_ref[...]
         pieces = functools.partial(dy_piece, cfg, e_ref, log_ref, lab_ref, lse_ref, xh_ref, dyt_ref, part_out)
 
         @pl.when(stage == helper)
         def _():
-            pieces(SPLIT_DY + DY_LATE, full, True)
+            pieces(SPLIT_DY + LATE_HELPER, full, True)
 
         @pl.when(stage != helper)
         def _():
-            pieces(DY_LATE, SPLIT_DY, False)
-
-        for c in range(groups + 1):
-            zero_copy(c).wait()
+            pieces(LATE_FIRST, SPLIT_DY, False)
+
+        for copy in zeros + smalls:
+            copy.wait()
 
 
 def sum_kernel(cfg, e_ref, log_ref, lab_ref, lse_ref, xh_ref, pin_ref, sum_out, part_ref, dyt_ref, got, send_sem, recv_sem):
@@ -513,12 +506,13 @@
     mids = helper
     bar = pltpu.get_barrier_semaphore()
 
-    def copy_to(to_stage, off, idx):
+    def copy_to(to_stage, off):
         slot = (stage - 1) * tps + rank
-        return pltpu.make_async_remote_copy(part_ref, got.at[slot], send_sem.at[idx], recv_sem.at[slot], device_id={'pp': to_stage, 'tp': lax.rem(rank + off, tps)}, device_id_type=MESH)
-
-    def arrived(slot):
-        return pltpu.make_async_remote_copy(part_ref, got.at[slot], send_sem.at[0], recv_sem.at[slot], device_id={'tp': rank}, device_id_type=MESH)
+        return pltpu.make_async_remote_copy(part_ref, got.at[slot], send_sem, recv_sem, device_id={'pp': to_stage, 'tp': lax.rem(rank + off, tps)}, device_id_type=MESH)
+
+    def batch(count):
+        some = got.at[pl.ds(0, count)]
+        return pltpu.make_async_remote_copy(some, some, send_sem, recv_sem, device_id={'tp': lax.rem(rank + 1, tps)}, device_id_type=MESH)
 
     def total(at):
         return functools.reduce(jnp.add, [got[at * tps + r] for r in range(tps)])
@@ -535,42 +529,35 @@
 
         @pl.when(stage == helper)
         def _():
-            pieces(SPLIT_DY, SPLIT_DY + DY_LATE, False)
+            pieces(SPLIT_DY, SPLIT_DY + LATE_HELPER, False)
 
         @pl.when(stage != helper)
         def _():
-            pieces(0, DY_LATE, False)
+            pieces(0, LATE_FIRST, False)
         pl.semaphore_wait(bar, mids * tps - 1)
 
         @pl.when(stage == helper)
         def _():
-            sends = [copy_to(helper, off, off) for off in range(1, tps)]
+            sends = [copy_to(helper, off) for off in range(1, tps)]
             for send in sends:
                 send.start()
             got[(helper - 1) * tps + rank] = part_ref[...]
-            for at in range(helper - 1):
-                for r in range(tps):
-                    arrived(at * tps + r).wait_recv()
-            for off in range(1, tps):
-                arrived((helper - 1) * tps + lax.rem(rank + off, tps)).wait_recv()
+            batch(mids * tps - 1).wait_recv()
             own = total(helper - 1)
             rest = functools.reduce(jnp.add, [total(at) for at in range(helper)])
             sum_out[...] = jnp.concatenate([own[0:2, :], rest[2:8, :]], axis=0)
-            for send in sends:
-                send.wait_send()
+            batch(tps - 1).wait_send()
 
         @pl.when(stage != helper)
         def _():
-            sends = [copy_to(helper, off, tps + off) for off in range(tps)] + [copy_to(stage, off, off) for off in range(1, tps)]
+            sends = [copy_to(helper, off) for off in range(tps)] + [copy_to(stage, off) for off in range(1, tps)]
             for send in sends:
                 send.start()
             mine = (stage - 1) * tps
             got[mine + rank] = part_ref[...]
-            for off in range(1, tps):
-                arrived(mine + lax.rem(rank + off, tps)).wait_recv()
+            batch(tps - 1).wait_recv()
             sum_out[...] = functools.reduce(jnp.add, [got[mine + r] for r in range(tps)])
-            for send in sends:
-                send.wait_send()
+            batch(2 * tps - 1).wait_send()
 
     @pl.when((stage == 0) | (stage == last))
     def _():
@@ -640,29 +627,28 @@
         cfg = (stages, tps, toks, dim, vocab)
         rows = toks + 2 * chunks
         vec = S((8, LANES), F)
-        weights = (S((dim, ff), F), S((1, ff), F), S((ff, dim), F))
+        weights = (S((dim, ff), F), S((ff, dim), F))
         mids = pl.pallas_call(
             functools.partial(stats_kernel, cfg), name='stats',
-            out_shape=(S((vocab, dim), B), S((vocab, toks), F), S((vocab, dim), F), S((toks, dim), B), S((8, LANES), I), vec, S((toks, dim), B), S((8, LANES), I), S((toks, dim), F), vec) + weights,
+            out_shape=(S((vocab, dim), B), S((vocab, toks), F), S((vocab, dim), F), S((toks, dim), B), S((8, LANES), I), vec, S((toks, dim), B), S((8, LANES), I), S((toks, dim), F), vec) + weights + (S((dim, toks), B),),
             in_specs=[hbm] * 9, out_specs=[vmem] * 13,
             scratch_shapes=[
                 V((chunks, LANES), I), V((toks, dim), B), V((toks, dim), B), V((1, dim), F), V((1, dim), F), V((dim, ff), B), V((1, ff), F), V((ff, dim), B), pltpu.SMEM((chunks, LANES), I),
-                V((dim, toks), B), V((2, TILE + 32, toks), F), V((rows, dim), F), V((rows, dim), F), V((rows, dim), F), V((rows, dim), F),
+                V((2, TILE + 32, toks), F), V((rows, dim), F), V((rows, dim), F), V((rows, dim), F), V((rows, dim), F),
                 V((8, LANES), F), V((2 * tps, 8, LANES), F), V((vocab, dim), F), V((toks, dim), F), V((8, LANES), F), V((tps, 8, LANES), F),
-                DMA((PARTS,)), DMA((9,)), DMA((4 + stages * tps,)), DMA((2,)), DMA, DMA((2 * tps,)), DMA((tps,))],
+                DMA((PARTS,)), DMA((9,)), DMA((4,)), DMA, DMA((2,)), DMA, DMA, DMA],
             compiler_params=pltpu.CompilerParams(collective_id=0, has_side_effects=True, vmem_limit_bytes=GRANT),
         )(*stay(ids, hid, cot, ln_gamma, ln_beta, table, w_in[0], b_in, w_out[0]))
-        groups = (vocab // TILE - 1) // 16 + 1
         emb_grad, w1g, b1g, w2g, part = pl.pallas_call(
             functools.partial(grad_kernel, cfg), name='grads',
-            out_shape=(S((vocab, dim), F),) + weights + (vec,),
-            in_specs=[vmem] * 13, out_specs=[hbm] + [vmem] * 4,
-            scratch_shapes=[V((vocab, dim), F), V((dim, toks), F), DMA((groups,))],
+            out_shape=(S((vocab, dim), F), S((dim, ff), F), S((1, ff), F), S((ff, dim), F), vec),
+            in_specs=[vmem] * 13, out_specs=[hbm] * 4 + [vmem],
+            scratch_shapes=[V((vocab, dim), F), V((dim, toks), F), V((dim, ff), F), V((1, ff), F), DMA((5,)), DMA((3,))],
             compiler_params=pltpu.CompilerParams(vmem_limit_bytes=GRANT),
         )(*mids)
         sums = pl.pallas_call(
             functools.partial(sum_kernel, cfg), name='sums', out_shape=vec, in_specs=[vmem] * 6, out_specs=vmem,
-            scratch_shapes=[V((8, LANES), F), V((dim, toks), F), V(((stages - 2) * tps, 8, LANES), F), DMA((2 * tps,)), DMA(((stages - 2) * tps,))],
+            scratch_shapes=[V((8, LANES), F), V((dim, toks), F), V(((stages - 2) * tps, 8, LANES), F), DMA, DMA],
             compiler_params=pltpu.CompilerParams(collective_id=1, has_side_effects=True, vmem_limit_bytes=GRANT),
         )(mids[0], mids[1], mids[4], mids[5], mids[8], part)
         vecs = pl.pallas_call(

time: 27.5 us -> 25.4 us (0.924)
  the two profiles are of different devices: /device:TPU:7 before, /device:TPU:0 now
where the time goes in v4:
time: 25.4 us; the launch traced here: 25.3 us
  Pallas kernels  24.4 us (96%)
  between operations  0.85 us (3%)
    pallas_call x1, Pallas kernels, body(): pl.pallas_call(functools.partial(stats_kernel, cfg), name='stats', out_sh...  15.4 us
    pallas_call x1, Pallas kernels, body(): pl.pallas_call(functools.partial(grad_kernel, cfg), name='grads', out_sha...  8.32 us
    pallas_call x1, Pallas kernels, body(): pl.pallas_call(write_kernel, name='write', out_shape=(S((1, dim), F), S((...  0.63 us

profile of v4, /device:TPU:0, one launch (start us, length us, event | category | flops | bytes accessed | tf_op | source)
XLA Modules:
  0.0 25.3 jit_solution(7849278932117256)
XLA Ops:
  0.6 15.4 %stats.1 = (bf16[12576,128]{1,0:T(8,128)(2,1)S(1)}, f32[12576,512]{1,0:T(8,128)S(1)}, f32[12576,128]{1,0:T(8,128)S(1)}, bf16[512,128]{1,0:T(8,128)(2,1)S(1)}, s3...) custom-call(s32[4,128]{1,0:T(4,128)} %bitcast.14, ...), custom_call_target="tpu_custom_call" | custom-call | tf_op jit(solution)/shard_map/stats/pallas_call | solution.py:631
  16.0 8.3 %grads.1 = (f32[12576,128]{1,0:T(8,128)}, f32[128,128]{1,0:T(8,128)}, f32[1,128]{1,0:T(1,128)}, f32[128,128]{1,0:T(8,128)}, f32[8,128]{1,0:T(8,128)S(1)}) custom-call(bf16[12576,128]{1,0:T(8,128)(2,1)S(1)} %get-tuple-element.28.e_ref, f32[12576,512]{1,0:T(8,128)S(1)} %get-tuple-element.29.log_ref, f32[12576,128]{1,0:T(8,128)S(1)} %get-tuple-element.30.first_ref, ...), custom_call_target="tpu_custom_call" | custom-call | tf_op jit(solution)/shard_map/grads/pallas_call | solution.py:642
  24.3 0.1 sums.1.sum_ref
  24.4 0.1 hand.1.vec_ref
  24.5 0.6 %write.1 = (f32[1,128]{1,0:T(1,128)}, f32[1,128]{1,0:T(1,128)}, f32[1]{0:T(128)}) custom-call(f32[8,128]{1,0:T(8,128)S(1)} %hand.1.vec_ref), custom_call_target="tpu_custom_call" | custom-call | tf_op jit(solution)/shard_map/write/pallas_call | solution.py:659

commit v5 on v4

--- a/solution.py
+++ b/solution.py
@@ -27,9 +27,17 @@
 TN = (((0,), (0,)), ((), ()))
 
 
+def col_sum(values):
+    return jnp.sum(values, axis=0, keepdims=True)
+
+
+def row_mean(values):
+    return jnp.mean(values, axis=-1, keepdims=True)
+
+
 def ln_hat(rows):
-    centre = rows - jnp.mean(rows, axis=-1, keepdims=True)
-    inv = lax.rsqrt(jnp.mean(centre * centre, axis=-1, keepdims=True) + LN_EPS)
+    centre = rows - row_mean(rows)
+    inv = lax.rsqrt(row_mean(centre * centre) + LN_EPS)
     return centre * inv, inv
 
 
@@ -55,10 +63,10 @@
 
 
 def stats_kernel(cfg, ids_hbm, hid_hbm, cot_hbm, gam_hbm, bet_hbm, emb_hbm, w1_hbm, b1_hbm, w2_hbm,
-                 e_ref, log_ref, first_ref, y_out, lab_out, lse_out, dx_out, did_out, xh_out, part_out, w1_out, w2_out, yt_ref,
+                 e_ref, log_ref, first_ref, y_out, lab_out, lse_out, dx_out, did_out, xh_out, part_out, w1_out, w2_out, yt_ref, tgt_out,
                  ids_ref, hid_ref, cot_ref, gam_ref, bet_ref, w1_ref, b1_ref, w2_ref, ids_smem,
-                 buf, pack_src, pack_dst, dx_src, dx_dst, st_src, st_all, e32_ref, x_ref, part_src, part_all,
-                 e_sem, in_sem, send_sem, many_sem, pack_sem, dx_sem, st_sem, part_sem):
+                 where_ref, where_smem, tgt_src, tgt_dst, buf, pack_src, pack_dst, dx_src, dx_dst, st_src, st_all, e32_ref, x_ref, part_src, part_all,
+                 e_sem, in_sem, send_sem, many_sem, pack_sem, dx_sem, st_sem, part_sem, tgt_sem):
     stages, tps, toks, dim, vocab = cfg
     chunks = toks // LANES
     rank = lax.axis_index('tp')
@@ -105,6 +113,29 @@
     def dx_copy():
         return remote(dx_src, dx_dst, send_sem.at[0], dx_sem, last)
 
+    where_ld = pltpu.make_async_copy(where_ref, where_smem, in_sem.at[5])
+
+    def tgt_copy():
+        return remote(tgt_src, tgt_dst, send_sem.at[4], tgt_sem, 0)
+
+    def label_logits():
+        place = lax.broadcasted_iota(jnp.int32, (8, LANES), 1) * 8 + lax.broadcasted_iota(jnp.int32, (8, LANES), 0)
+        where_ld.wait()
+
+        def take(i, picked):
+            out = []
+            for c in range(chunks):
+                top = where_smem[c, i] * 8
+                out.append(jnp.where(place == where_smem[chunks + c, i], log_ref[pl.ds(top, 8), c * LANES:(c + 1) * LANES], picked[c]))
+            return tuple(out)
+
+        picked = lax.fori_loop(0, LANES, take, tuple(jnp.zeros((8, LANES), F) for _ in range(chunks)), unroll=8)
+        for c in range(chunks):
+            tgt_src[c:c + 1, :] = col_sum(picked[c])
+        tgt_src[chunks:8, :] = jnp.zeros((8 - chunks, LANES), F)
+        tgt_out[...] = tgt_src[...]
+        tgt_copy().start()
+
     def part_copy(off):
         return remote(part_src, part_all.at[rank], many_sem, part_sem, 0, off)
 
@@ -129,7 +160,7 @@
         start = which * half
         normed(pack_dst[vecs + start:vecs + start + half, :], pack_dst[chunks:chunks + 1, :], pack_dst[chunks + 1:chunks + 2, :], start, half)
         if which == 0:
-            lab_out[0:chunks, :] = pack_dst[0:chunks, :].astype(jnp.int32)
+            lab_out[:chunks, :] = pack_dst[:chunks, :].astype(jnp.int32)
 
     def unpack_all():
         for w in range(2):
@@ -153,7 +184,7 @@
         sums = [st_all[r, chunks:2 * chunks, :] for r in range(2 * tps)]
         top = functools.reduce(jnp.maximum, tops)
         tot = functools.reduce(jnp.add, [s * jnp.exp(t - top) for s, t in zip(sums, tops)])
-        lse_out[0:chunks, :] = top + jnp.log(tot)
+        lse_out[:chunks, :] = top + jnp.log(tot)
 
     def logit_tile(row, size):
         logits = mm(e_ref[pl.ds(row, size), :], yt_ref[...])
@@ -209,7 +240,7 @@
 
     def share_stats(top, tot, which):
         high = jnp.max(top, axis=0, keepdims=True)
-        tot = jnp.sum(tot * jnp.exp(top - high), axis=0, keepdims=True)
+        tot = col_sum(tot * jnp.exp(top - high))
         for c in range(chunks):
             st_src[c:c + 1, :] = high[:, c * LANES:(c + 1) * LANES]
             st_src[chunks + c:chunks + c + 1, :] = tot[:, c * LANES:(c + 1) * LANES]
@@ -231,10 +262,10 @@
         d_pre = d_act * slope
         d_b = d_pre.astype(B)
         w1_out[...] = lax.dot_general(norm, d_b, TN, preferred_element_type=F)
-        part_out[5:6, :] = jnp.sum(d_pre, axis=0, keepdims=True)
+        part_out[5:6, :] = col_sum(d_pre)
         d_h = lax.dot_general(d_b, w1_ref[...], NT, preferred_element_type=F)
-        part_out[0:1, :] = jnp.sum(d_h * hat, axis=0, keepdims=True)
-        part_out[1:2, :] = jnp.sum(d_h, axis=0, keepdims=True)
+        part_out[0:1, :] = col_sum(d_h * hat)
+        part_out[1:2, :] = col_sum(d_h)
         part_out[2:5, :] = jnp.zeros((3, LANES), F)
         part_out[6:8, :] = jnp.zeros((2, LANES), F)
 
@@ -246,13 +277,17 @@
         fetch(*e_parts[1:])
         rows = hid_ref[...].astype(F)
         pack_src[vecs:vecs + toks, :] = rows
-        pack_src[0:chunks, :] = ids_ref[...].astype(F)
+        pack_src[:chunks, :] = ids_ref[...].astype(F)
         pack_src[chunks:chunks + 1, :] = gam_ref[...]
         pack_src[chunks + 1:chunks + 2, :] = bet_ref[...]
         pack_src[chunks + 2:vecs, :] = jnp.zeros((vecs - chunks - 2, dim), F)
         normed(rows, gam_ref[...], bet_ref[...], 0, toks)
-        lab_out[0:chunks, :] = ids_ref[...]
+        lab_out[:chunks, :] = ids_ref[...]
         e_parts[0].wait()
+        row = jnp.clip(ids_ref[...] - rank * vocab, 0, vocab - 1)
+        where_ref[:chunks, :] = row >> 3
+        where_ref[chunks:2 * chunks, :] = lax.broadcasted_iota(jnp.int32, (chunks, LANES), 1) * 8 + (row & 7)
+        where_ld.start()
         carry = run_stats(0, EARLY // 2, begin_stats(0))
         met()
         packs = pack_sends()
@@ -264,14 +299,16 @@
         share_stats(top, tot, 0)
         fill_logits(SPLIT_STATS, full)
         logit_tile(full * TILE, tail)
+        label_logits()
         dx_copy().wait_recv()
-        dx_out[...] = dx_dst[0:toks, :].astype(B)
-        did_out[0:chunks, :] = dx_dst[toks:toks + chunks, :].astype(jnp.int32)
+        dx_out[...] = dx_dst[:toks, :].astype(B)
+        did_out[:chunks, :] = dx_dst[toks:toks + chunks, :].astype(jnp.int32)
         first_tiles(0, FIRST)
         st_wait(2 * tps - 1)
         finish_stats()
         for send in packs:
             send.wait_send()
+        tgt_copy().wait_send()
         st_sent()
 
     @pl.when(stage == helper)
@@ -320,14 +357,14 @@
         hat, inv = ln_hat(x_ref[...])
         cot = cot_ref[...].astype(F)
         scaled = cot * gam_ref[...]
-        grad = inv * (scaled - jnp.mean(scaled, axis=-1, keepdims=True) - hat * jnp.mean(scaled * hat, axis=-1, keepdims=True))
+        grad = inv * (scaled - row_mean(scaled) - hat * row_mean(scaled * hat))
         grad = jnp.where(mask > 0.5, grad, 0.0).astype(B)
         dx_out[...] = grad
-        did_out[0:chunks, :] = ids_ref[...]
-        dx_src[0:toks, :] = grad.astype(F)
+        did_out[:chunks, :] = ids_ref[...]
+        dx_src[:toks, :] = grad.astype(F)
         dx_src[toks:toks + chunks, :] = ids_ref[...].astype(F)
-        part_src[0:1, :] = jnp.sum(jnp.where(mask > 0.5, cot * hat, 0.0), axis=0, keepdims=True)
-        part_src[1:2, :] = jnp.sum(jnp.where(mask > 0.5, cot, 0.0), axis=0, keepdims=True)
+        part_src[0:1, :] = col_sum(jnp.where(mask > 0.5, cot * hat, 0.0))
+        part_src[1:2, :] = col_sum(jnp.where(mask > 0.5, cot, 0.0))
         part_src[2:8, :] = jnp.zeros((6, LANES), F)
         part_all[rank] = part_src[...]
         met()
@@ -344,6 +381,8 @@
         logit_tile(full * TILE, tail)
         others = part_all.at[pl.ds(0, tps - 1)]
         remote(others, others, many_sem, part_sem, 0, 1).wait_recv()
+        tgt_copy().wait_recv()
+        tgt_out[...] = tgt_dst[...]
         part_out[...] = functools.reduce(jnp.add, [part_all[r] for r in range(tps)])
         st_wait(2 * tps)
         finish_stats()
@@ -397,12 +436,12 @@
         seen = work(full * TILE, tail, seen)
     loss = functools.reduce(jnp.add, seen)
     dy = dyt_ref[...].T
-    part_ref[2:3, :] += jnp.sum(dy * xh_ref[...], axis=0, keepdims=True)
-    part_ref[3:4, :] += jnp.sum(dy, axis=0, keepdims=True)
-    part_ref[4:5, :] += jnp.sum(loss, axis=0, keepdims=True)
-
-
-def grad_kernel(cfg, e_ref, log_ref, first_ref, y_ref, lab_ref, lse_ref, dx_ref, did_ref, xh_ref, pin_ref, w1_in, w2_in, yt_ref,
+    part_ref[2:3, :] += col_sum(dy * xh_ref[...])
+    part_ref[3:4, :] += col_sum(dy)
+    part_ref[4:5, :] += col_sum(loss)
+
+
+def grad_kernel(cfg, e_ref, log_ref, first_ref, y_ref, lab_ref, lse_ref, dx_ref, did_ref, xh_ref, pin_ref, w1_in, w2_in, yt_ref, tgt_ref,
                 emb_out, w1_out, b1_out, w2_out, part_out, out_ref, dyt_ref, zero_ref, bias_ref, o_sem, w_sem):
     stages, tps, toks, dim, vocab = cfg
     chunks = toks // LANES
@@ -430,6 +469,8 @@
         lse = lanes_row(lse_ref, 0, chunks)
         lab = local_ids(lab_ref, chunks, base, vocab)
         did = local_ids(did_ref, chunks, base, vocab)
+        less = jnp.exp2((lanes_row(tgt_ref, 0, chunks) - lse) * LOG2E) - 1.0
+        less = [jnp.broadcast_to(less[:, c * LANES:(c + 1) * LANES], (16, LANES)).astype(B) for c in range(chunks)]
 
         def out_copy(c):
             start, size = (full * TILE, tail) if c == len(spans) else (spans[c][0] * TILE, (spans[c][1] - spans[c][0]) * TILE)
@@ -443,8 +484,8 @@
             g, h = [], []
             for c in range(chunks):
                 cols = slice(c * LANES, (c + 1) * LANES)
-                pc = p[:, cols]
-                g.append(jnp.where(rows == lab[:, cols], (pc - 1.0).astype(B), pc.astype(B)))
+                hit = jnp.concatenate([less[c]] * (size // 16), axis=0)
+                g.append(jnp.where(rows == lab[:, cols], hit, p[:, cols].astype(B)))
                 if pick:
                     h.append(jnp.where(rows == did[:, cols], one, zero))
             first = mm(jnp.concatenate(h, axis=1), dx_ref[...]) if pick else first_ref[pl.ds(row, size), :]
@@ -630,19 +671,19 @@
         weights = (S((dim, ff), F), S((ff, dim), F))
         mids = pl.pallas_call(
             functools.partial(stats_kernel, cfg), name='stats',
-            out_shape=(S((vocab, dim), B), S((vocab, toks), F), S((vocab, dim), F), S((toks, dim), B), S((8, LANES), I), vec, S((toks, dim), B), S((8, LANES), I), S((toks, dim), F), vec) + weights + (S((dim, toks), B),),
-            in_specs=[hbm] * 9, out_specs=[vmem] * 13,
+            out_shape=(S((vocab, dim), B), S((vocab, toks), F), S((vocab, dim), F), S((toks, dim), B), S((8, LANES), I), vec, S((toks, dim), B), S((8, LANES), I), S((toks, dim), F), vec) + weights + (S((dim, toks), B), vec),
+            in_specs=[hbm] * 9, out_specs=[vmem] * 14,
             scratch_shapes=[
                 V((chunks, LANES), I), V((toks, dim), B), V((toks, dim), B), V((1, dim), F), V((1, dim), F), V((dim, ff), B), V((1, ff), F), V((ff, dim), B), pltpu.SMEM((chunks, LANES), I),
-                V((2, TILE + 32, toks), F), V((rows, dim), F), V((rows, dim), F), V((rows, dim), F), V((rows, dim), F),
+                V((2 * chunks, LANES), I), pltpu.SMEM((2 * chunks, LANES), I), V((8, LANES), F), V((8, LANES), F), V((2, TILE + 32, toks), F), V((rows, dim), F), V((rows, dim), F), V((rows, dim), F), V((rows, dim), F),
                 V((8, LANES), F), V((2 * tps, 8, LANES), F), V((vocab, dim), F), V((toks, dim), F), V((8, LANES), F), V((tps, 8, LANES), F),
-                DMA((PARTS,)), DMA((9,)), DMA((4,)), DMA, DMA((2,)), DMA, DMA, DMA],
+                DMA((PARTS,)), DMA((9,)), DMA((5,)), DMA, DMA((2,)), DMA, DMA, DMA, DMA],
             compiler_params=pltpu.CompilerParams(collective_id=0, has_side_effects=True, vmem_limit_bytes=GRANT),
         )(*stay(ids, hid, cot, ln_gamma, ln_beta, table, w_in[0], b_in, w_out[0]))
         emb_grad, w1g, b1g, w2g, part = pl.pallas_call(
             functools.partial(grad_kernel, cfg), name='grads',
             out_shape=(S((vocab, dim), F), S((dim, ff), F), S((1, ff), F), S((ff, dim), F), vec),
-            in_specs=[vmem] * 13, out_specs=[hbm] * 4 + [vmem],
+            in_specs=[vmem] * 14, out_specs=[hbm] * 4 + [vmem],
             scratch_shapes=[V((vocab, dim), F), V((dim, toks), F), V((dim, ff), F), V((1, ff), F), DMA((5,)), DMA((3,))],
             compiler_params=pltpu.CompilerParams(vmem_limit_bytes=GRANT),
         )(*mids)
@@ -662,6 +703,7 @@
         )(vecs)
         return emb_grad[None], loss, gam, bet, w1g[None], b1g, w2g[None]
 
-    specs_in = (P(lead, None, None), P(lead, None, None, None), P(lead, None, None, None), P(lead, None), P(lead, None), P(lead, 'tp', None), P(lead, None, 'tp'), P(lead, 'tp'), P(lead, 'tp', None))
-    specs_out = (P(lead, 'tp', None), P(lead), P(lead, None), P(lead, None), P(lead, None, 'tp'), P(lead, 'tp'), P(lead, 'tp', None))
+    rows, cols = P(lead, 'tp'), P(lead, None, 'tp')
+    specs_in = (P(lead),) * 5 + (rows, cols, rows, rows)
+    specs_out = (rows, P(lead), P(lead), P(lead), cols, rows, rows)
     return jax.shard_map(body, mesh=mesh, in_specs=specs_in, out_specs=specs_out, check_vma=False)

time: 25.4 us -> 24.5 us (0.965)
  the two profiles are of different devices: /device:TPU:0 before, /device:TPU:7 now
where the time goes in v5:
time: 24.5 us; the launch traced here: 24.3 us
  Pallas kernels  23.5 us (96%)
  between operations  0.85 us (3%)
    pallas_call x1, Pallas kernels, body(): pl.pallas_call(functools.partial(stats_kernel, cfg), name='stats', out_sh...  12.1 us
    pallas_call x1, Pallas kernels, body(): pl.pallas_call(functools.partial(grad_kernel, cfg), name='grads', out_sha...  8.49 us
    pallas_call x1, Pallas kernels, body(): pl.pallas_call(functools.partial(hand_kernel, cfg), name='hand', out_shap...  2.13 us
    pallas_call x1, Pallas kernels, body(): pl.pallas_call(write_kernel, name='write', out_shape=(S((1, dim), F), S((...  0.63 us

profile of v5, /device:TPU:7, one launch (start us, length us, event | category | flops | bytes accessed | tf_op | source)
XLA Modules:
  0.0 24.3 jit_solution(6983890777265291659)
XLA Ops:
  0.6 12.1 %stats.1 = (bf16[12576,128]{1,0:T(8,128)(2,1)S(1)}, f32[12576,512]{1,0:T(8,128)S(1)}, f32[12576,128]{1,0:T(8,128)S(1)}, bf16[512,128]{1,0:T(8,128)(2,1)S(1)}, s3...) custom-call(s32[4,128]{1,0:T(4,128)} %bitcast.14, ...), custom_call_target="tpu_custom_call" | custom-call | tf_op jit(solution)/shard_map/stats/pallas_call | solution.py:672
  12.8 8.5 %grads.1 = (f32[12576,128]{1,0:T(8,128)}, f32[128,128]{1,0:T(8,128)}, f32[1,128]{1,0:T(1,128)}, f32[128,128]{1,0:T(8,128)}, f32[8,128]{1,0:T(8,128)S(1)}) custom-call(bf16[12576,128]{1,0:T(8,128)(2,1)S(1)} %get-tuple-element.29.e_ref, f32[12576,512]{1,0:T(8,128)S(1)} %get-tuple-element.30.log_ref, f32[12576,128]{1,0:T(8,128)S(1)} %get-tuple-element.31.first_ref, ...), custom_call_target="tpu_custom_call" | custom-call | tf_op jit(solution)/shard_map/grads/pallas_call | solution.py:683
  21.3 0.1 sums.1.sum_ref
  21.4 2.1 %hand.1.vec_ref = f32[8,128]{1,0:T(8,128)S(1)} custom-call(f32[8,128]{1,0:T(8,128)S(1)} %sums.1.sum_ref), custom_call_target="tpu_custom_call" | custom-call | tf_op jit(solution)/shard_map/hand/pallas_call | solution.py:695
  23.5 0.6 %write.1 = (f32[1,128]{1,0:T(1,128)}, f32[1,128]{1,0:T(1,128)}, f32[1]{0:T(128)}) custom-call(f32[8,128]{1,0:T(8,128)S(1)} %hand.1.vec_ref), custom_call_target="tpu_custom_call" | custom-call | tf_op jit(solution)/shard_map/write/pallas_call | solution.py:700

commit v6 on v5

--- a/solution.py
+++ b/solution.py
@@ -14,13 +14,13 @@
 LANES = 128
 TILE = 256
 SPLIT_STATS = 37
-SPLIT_DY = 16
+SPLIT_DY = 20
 EARLY = 8
 FIRST = 16
 FRESH = 48
 PARTS = 4
-LATE_HELPER = 16
-LATE_FIRST = 6
+LATE_HELPER = 12
+LATE_FIRST = 8
 GRANT = 14 << 20
 MESH = pl.DeviceIdType.MESH
 NT = (((1,), (1,)), ((), ()))

time: 24.5 us -> 24.6 us (level)
  no operation moved by 1% of the time
where the time goes in v6:
time: 24.6 us; the launch traced here: 24.4 us
  Pallas kernels  23.6 us (96%)
  between operations  0.85 us (3%)
    pallas_call x1, Pallas kernels, body(): pl.pallas_call(functools.partial(stats_kernel, cfg), name='stats', out_sh...  12.1 us
    pallas_call x1, Pallas kernels, body(): pl.pallas_call(functools.partial(grad_kernel, cfg), name='grads', out_sha...  8.49 us
    pallas_call x1, Pallas kernels, body(): pl.pallas_call(functools.partial(hand_kernel, cfg), name='hand', out_shap...  2.23 us
    pallas_call x1, Pallas kernels, body(): pl.pallas_call(write_kernel, name='write', out_shape=(S((1, dim), F), S((...  0.63 us

profile of v6, /device:TPU:7, one launch (start us, length us, event | category | flops | bytes accessed | tf_op | source)
XLA Modules:
  0.0 24.4 jit_solution(1030363205565499664)
XLA Ops:
  0.6 12.1 %stats.1 = (bf16[12576,128]{1,0:T(8,128)(2,1)S(1)}, f32[12576,512]{1,0:T(8,128)S(1)}, f32[12576,128]{1,0:T(8,128)S(1)}, bf16[512,128]{1,0:T(8,128)(2,1)S(1)}, s3...) custom-call(s32[4,128]{1,0:T(4,128)} %bitcast.14, ...), custom_call_target="tpu_custom_call" | custom-call | tf_op jit(solution)/shard_map/stats/pallas_call | solution.py:672
  12.8 8.5 %grads.1 = (f32[12576,128]{1,0:T(8,128)}, f32[128,128]{1,0:T(8,128)}, f32[1,128]{1,0:T(1,128)}, f32[128,128]{1,0:T(8,128)}, f32[8,128]{1,0:T(8,128)S(1)}) custom-call(bf16[12576,128]{1,0:T(8,128)(2,1)S(1)} %get-tuple-element.29.e_ref, f32[12576,512]{1,0:T(8,128)S(1)} %get-tuple-element.30.log_ref, f32[12576,128]{1,0:T(8,128)S(1)} %get-tuple-element.31.first_ref, ...), custom_call_target="tpu_custom_call" | custom-call | tf_op jit(solution)/shard_map/grads/pallas_call | solution.py:683
  21.3 0.1 sums.1.sum_ref
  21.4 2.2 %hand.1.vec_ref = f32[8,128]{1,0:T(8,128)S(1)} custom-call(f32[8,128]{1,0:T(8,128)S(1)} %sums.1.sum_ref), custom_call_target="tpu_custom_call" | custom-call | tf_op jit(solution)/shard_map/hand/pallas_call | solution.py:695
  23.6 0.6 %write.1 = (f32[1,128]{1,0:T(1,128)}, f32[1,128]{1,0:T(1,128)}, f32[1]{0:T(128)}) custom-call(f32[8,128]{1,0:T(8,128)S(1)} %hand.1.vec_ref), custom_call_target="tpu_custom_call" | custom-call | tf_op jit(solution)/shard_map/write/pallas_call | solution.py:700
